TPU v7x, 32 devices: a whole 2x2x4 slice. The times are simulated.
32 devices in a mesh: wide: 8 (over z, x), narrow: 4 (over y, core).
Axes of the slice: x: 2, y: 2, z: 4, core: 2. Of those that a mesh axis runs over, the one named last changes fastest.
Arguments:
- activations: bfloat16 [2048, 16384], P('wide', 'narrow'), may hold values from -6 to 6
- grad_out: bfloat16 [2048, 8192], P('narrow', 'wide'), may hold values from -0.125 to 0.125
- momentum: float32 [8192, 16384], P('wide', 'narrow'), may hold values from -90 to 90
- right_factor: float32 [16384, 512], P('narrow'), may hold values from -0.046875 to 0.046875
Outputs:
- new_momentum: float32 [8192, 16384], P('wide', 'narrow')
- new_right: float32 [16384, 512], P('narrow')
- update: bfloat16 [8192, 16384], P('wide', 'narrow')
All inputs are finite; a program needn't handle non-finite values.
Results may differ from a plain program's by a relative error of at most 0.0012.
Values may be sent and summed in bfloat16 or wider, within the bound.
No kernel may reach another device: no remote copies, remote signals or barrier semaphores. Data moves between devices by JAX's collectives and lax.ppermute only.
A program may use at most 128 MiB of HBM per device.

v0:
```python
import math

import jax
import jax.numpy as jnp
from jax import lax
from jax.sharding import PartitionSpec as P

DOUT = 8192
DIN = 16384
RANK = 512


FEEDBACK = 0.05
EPSILON = 1e-06


def body(activations, grad_out, momentum, right_factor):
    highest = lax.Precision.HIGHEST
    out_rows = lax.all_gather(grad_out, "narrow", axis=0, tiled=True)
    gradient = lax.dot_general(
        out_rows,
        lax.all_gather(activations, "wide", axis=0, tiled=True),
        (((0,), (0,)), ((), ())),
        preferred_element_type=jnp.float32,
    )
    buffer = momentum + gradient
    partial_left = jnp.dot(
        buffer, right_factor, precision=highest, preferred_element_type=jnp.float32
    )
    left_factor = lax.psum(partial_left, "narrow")
    gram_local = jnp.dot(
        left_factor.T, left_factor, precision=highest, preferred_element_type=jnp.float32
    )
    gram_matrix = lax.psum(gram_local, "wide")
    lower_factor = jnp.linalg.cholesky(gram_matrix)
    ortho_left = jax.scipy.linalg.solve_triangular(lower_factor, left_factor.T, lower=True).T
    right_share = lax.psum_scatter(
        lax.dot_general(
            buffer,
            ortho_left,
            (((0,), (0,)), ((), ())),
            precision=highest,
            preferred_element_type=jnp.float32,
        ),
        "wide",
        scatter_dimension=0,
        tiled=True,
    )
    col_squares = lax.psum(jnp.sum(right_share * right_share, axis=0), ("wide", "narrow"))
    right_raw = lax.all_gather(right_share, "wide", axis=0, tiled=True)
    feedback = lax.dot_general(
        ortho_left,
        right_raw,
        (((1,), (1,)), ((), ())),
        precision=highest,
        preferred_element_type=jnp.float32,
    )
    new_momentum = buffer - FEEDBACK * feedback
    new_right = right_raw / (jnp.sqrt(col_squares) + EPSILON)
    update_scale = math.sqrt(DOUT * DIN / RANK)
    product = lax.dot_general(
        ortho_left,
        new_right,
        (((1,), (1,)), ((), ())),
        precision=highest,
        preferred_element_type=jnp.float32,
    )
    update = (update_scale * product).astype(jnp.bfloat16)
    return (new_momentum, new_right, update)


def solution(mesh):
    return jax.shard_map(
        body,
        mesh=mesh,
        in_specs=(P("wide", "narrow"), P("narrow", "wide"), P("wide", "narrow"), P("narrow", None)),
        out_specs=(P("wide", "narrow"), P("narrow", None), P("wide", "narrow")),
        check_vma=False,
    )
```

profile of v0, /device:TPU:0, one launch (start us, length us, event | category | flops | bytes accessed | tf_op | source)
XLA Modules:
  0.0 1089.3 jit_solution(18141778755275494876)
XLA Ops:
  7.2 0.7 all-gather.4.cloned.1.call-update
  7.9 0.7 all-gather.6.cloned.1.call-update
  8.7 38.1 %all-gather.4.cloned.1.call-done = bf16[2048,1024]{1,0:T(8,128)(2,1)} async-done(((bf16[512,1024]{1,0:T(8,128)(2,1)}), bf16[2048,1024]{1,0:T(8,128)(2,1)}) %all-gather.4.cloned.1.call-update) | async-done | bytes 4194320 | tf_op jit(solution)/shard_map/all_gather | solution.py:19
  46.7 229.4 %all-gather.6.cloned.1.call-done = bf16[2048,4096]{1,0:T(8,128)(2,1)} async-done(((bf16[256,4096]{1,0:T(8,128)(2,1)}), bf16[2048,4096]{1,0:T(8,128)(2,1)}) %all-gather.6.cloned.1.call-update) | async-done | bytes 16777232 | tf_op jit(solution)/shard_map/all_gather | solution.py:22
  276.2 28.3 %convolution_add_fusion = f32[1024,4096]{1,0:T(8,128)} fusion(f32[1024,4096]{1,0:T(8,128)} %param.6, bf16[2048,1024]{1,0:T(8,128)(2,1)} %all-gather.4.cloned.1.call-done, bf16[2048,4096]{1,0:T(8,128)(2,1)} %all-gather.6.cloned.1.call-done), kind=kOutput, calls=%fused_computation.4 | convolution fusion | flops 17184063488 | bytes 54525952 | tf_op jit(solution)/shard_map/dot_general | solution.py:20
  304.5 31.4 %fusion.39 = f32[1024,512]{1,0:T(8,128)} fusion(f32[1024,4096]{1,0:T(8,128)} %convolution_add_fusion, f32[4096,512]{1,0:T(8,128)} %param.7), kind=kOutput, calls=%fused_computation.78 | convolution fusion | flops 25769803776 | bytes 27262976 | tf_op jit(solution)/shard_map/dot_general | solution.py:27
  336.0 49.7 %all-reduce.4.cloned.1.call-done = f32[1024,512]{1,0:T(8,128)} async-done(((f32[1024,512]{1,0:T(8,128)}), f32[1024,512]{1,0:T(8,128)}) %all-reduce.4.cloned.1.call-update) | async-done | bytes 2097168 | tf_op jit(solution)/shard_map/psum | solution.py:30
  385.6 6.7 fusion.40
  392.6 78.3 %all-reduce.6.cloned.1.call-done = f32[512,512]{0,1:T(8,128)} async-done(((f32[512,512]{0,1:T(8,128)}), f32[512,512]{0,1:T(8,128)}) %all-reduce.6.cloned.1.call-update) | async-done | bytes 1048592 | tf_op jit(solution)/shard_map/psum | solution.py:34
  470.9 1.6 copy.8
  472.5 1.4 fusion.12
  473.9 1.0 copy-done.3
  474.9 11.7 %cholesky.104 = f32[128,128]{1,0:T(8,128)S(1)} custom-call(f32[128,128]{1,0:T(8,128)S(1)} %cholesky.266), custom_call_target="Cholesky" | custom-call | tf_op jit(solution)/shard_map/jit(cholesky)/cholesky | solution.py:35
  486.8 9.8 custom-call.31
  496.6 1.2 constant_dynamic-update-slice_fusion.3
  497.8 1.3 convolution_subtract_fusion.2
  499.1 11.7 %cholesky.217 = f32[128,128]{1,0:T(8,128)S(1)} custom-call(f32[128,128]{1,0:T(8,128)S(1)} %cholesky.270), custom_call_target="Cholesky" | custom-call | tf_op jit(solution)/shard_map/jit(cholesky)/cholesky | solution.py:35
  510.9 10.0 custom-call.32
  521.1 1.3 convolution_subtract_fusion.3
  522.5 11.7 %cholesky.238 = f32[128,128]{1,0:T(8,128)S(1)} custom-call(f32[128,128]{1,0:T(8,128)S(1)} %cholesky.275), custom_call_target="Cholesky" | custom-call | tf_op jit(solution)/shard_map/jit(cholesky)/cholesky | solution.py:35
  534.2 9.8 custom-call.33
  544.2 1.2 convolution_subtract_fusion.4
  545.5 11.7 %cholesky.255 = f32[128,128]{1,0:T(8,128)S(1)} custom-call(f32[128,128]{1,0:T(8,128)S(1)} %convolution_subtract_fusion.4), custom_call_target="Cholesky" | custom-call | tf_op jit(solution)/shard_map/jit(cholesky)/cholesky | solution.py:35
  557.2 0.7 compare_reduce_fusion.1
  558.5 0.7 compare_reduce_fusion.2
  561.7 1.6 select_select_fusion
  563.3 13.6 %while.1 = (s32[]{:T(128)}, f32[512,512]{1,0:T(8,128)}, s32[4,2]{0,1:T(2,128)S(1)}, f32[4,128,128]{2,1,0:T(8,128)}, s32[]{:T(128)}) while((s32[]{:T(128)}, f32[512,512]{1,0:T(8,128)}, s32[4,2]{0,1:T(2,128)S(1)}, f32[4,128,128]{2,1,0:T(8,128)}, s32[]{:T(128)}) %tuple.31), condition=%wide.while_cond, body=%wide.while_body.sunk | while | flops 2 | bytes 132205 | solution.py:36
  563.9 2.8 bitcast_dynamic-update-slice_fusion.2
  567.3 2.8 bitcast_dynamic-update-slice_fusion.2
  570.7 2.8 bitcast_dynamic-update-slice_fusion.2
  574.1 2.8 bitcast_dynamic-update-slice_fusion.2
  576.9 40.1 %custom-call.34 = f32[4,128,128]{1,2,0:T(8,128)S(1)} custom-call(f32[4,128,128]{2,1,0:T(8,128)} %get-tuple-element.10), custom_call_target="InvertDiagBlocksLowerTriangular" | custom-call | tf_op jit(solution)/shard_map/jit(_solve_triangular)/triangular_solve | solution.py:36
  617.0 0.6 fusion.13
  617.7 1.8 convolution_subtract_fusion.1
  619.5 0.6 fusion.27
  620.2 2.9 convolution_subtract_fusion
  623.0 0.6 fusion.25
  623.7 3.8 fusion.6
  627.5 0.6 fusion.24
  628.2 0.8 copy-done.4
  629.0 56.3 %fusion.15 = f32[4096,512]{1,0:T(8,128)} fusion(f32[1024,4096]{1,0:T(8,128)} %convolution_add_fusion, f32[128,1024]{1,0:T(8,128)S(1)} %fusion.24, f32[128,1024]{1,0:T(8,128)S(1)} %fusion.25, f32[128,1024]{1,0:T(8,128)S(1)} %fusion.27, f32[128,1024]{1,0:T(8,128)S(1)} %fusion.13), kind=kOutput, calls=%fused_computation.31 | convolution fusion | flops 25771376640 | bytes 27262976 | tf_op jit(solution)/shard_map/dot_general | solution.py:38
  685.4 147.2 %reduce-scatter.2.cloned.1.call-done = f32[512,512]{1,0:T(8,128)} async-done(((f32[4096,512]{1,0:T(8,128)}), f32[512,512]{1,0:T(8,128)}) %reduce-scatter.2.cloned.1.call-update) | async-done | bytes 1048592 | tf_op jit(solution)/shard_map/reduce_scatter | solution.py:37
  832.6 1.3 multiply_reduce_fusion
  833.9 43.3 %psum.23 = f32[512]{0:T(512)S(1)} all-reduce(f32[512]{0:T(512)S(1)} %multiply_reduce_fusion), channel_id=1, replica_groups=mesh['wide'=8,'narrow'=4] {'wide','narrow'}, use_global_device_ids=true, to_apply=%region_12.13 | all-reduce | flops 512 | bytes 4096 | tf_op jit(solution)/shard_map/psum | solution.py:49
  877.2 82.0 %all-gather.8.cloned.1.call-done = f32[4096,512]{1,0:T(8,128)} async-done(((f32[512,512]{1,0:T(8,128)}), f32[4096,512]{1,0:T(8,128)}) %all-gather.8.cloned.1.call-update) | async-done | bytes 8388624 | tf_op jit(solution)/shard_map/all_gather | solution.py:50
  959.2 8.9 broadcast_divide_fusion
  968.1 56.8 %multiply_convert_fusion = bf16[1024,4096]{1,0:T(8,128)(2,1)} fusion(f32[4096,512]{1,0:T(8,128)} %broadcast_divide_fusion, f32[128,1024]{1,0:T(8,128)} %copy-done.4, f32[128,1024]{1,0:T(8,128)} %copy-done.2, f32[128,1024]{1,0:T(8,128)} %copy-done.1, f32[128,1024]{1,0:T(8,128)S(1)} %fusion.13), kind=kOutput, calls=%fused_computation.2 | convolution fusion | flops 25779765248 | bytes 18874368 | tf_op jit(solution)/shard_map/dot_general | solution.py:61
  1025.0 57.3 %multiply_subtract_fusion = f32[1024,4096]{1,0:T(8,128)} fusion(f32[1024,4096]{1,0:T(8,128)S(1)} %bitcast.65, f32[4096,512]{1,0:T(8,128)S(1)} %bitcast.59, f32[128,1024]{1,0:T(8,128)} %copy-done.4, f32[128,1024]{1,0:T(8,128)} %copy-done.2, f32[128,1024]{1,0:T(8,128)} %copy-done.1, f32[128,1024]{1,0:T(8,128)S(1)} %fusion.13), kind=kOutput, calls=%fused_computation.3 | convolution fusion | flops 25779765248 | bytes 44040192 | tf_op jit(solution)/shard_map/dot_general | solution.py:51
  (55 shorter events, 4.3 us)
Async XLA Ops:
  7.2 39.6 %all-gather.4.cloned.1.call-start = ((), (), s32[]{:S(2)}) async-start(), calls=%async_computation.1 | async-start | bytes 5242880 | tf_op jit(solution)/shard_map/all_gather | solution.py:19
  7.9 268.3 %all-gather.6.cloned.1.call-start = ((), (), s32[]{:S(2)}) async-start(), calls=%async_computation.2 | async-start | bytes 18874368 | tf_op jit(solution)/shard_map/all_gather | solution.py:22
  8.6 377.0 %all-reduce.4.cloned.1.call-start = ((), (), s32[]{:S(2)}) async-start(), calls=%async_computation.3 | async-start | bytes 4194304 | tf_op jit(solution)/shard_map/psum | solution.py:30
  335.9 135.0 %all-reduce.6.cloned.1.call-start = ((), (), s32[]{:S(2)}) async-start(), calls=%async_computation.4 | async-start | bytes 2097152 | tf_op jit(solution)/shard_map/psum | solution.py:34
  392.4 440.2 %reduce-scatter.2.cloned.1.call-start = ((), (), s32[]{:S(2)}) async-start(), calls=%async_computation.5 | async-start | bytes 9437184 | tf_op jit(solution)/shard_map/reduce_scatter | solution.py:37
  473.9 1.0 copy-start.3
  474.9 142.1 %copy-start = (f32[1024,512]{1,0:T(8,128)S(1)}, f32[1024,512]{1,0:T(8,128)}, u32[]{:S(2)}) copy-start(f32[1024,512]{1,0:T(8,128)} %all-reduce.4.cloned.1.call-done) | copy-start | bytes 6291460
  620.2 65.1 %copy-start.1 = (f32[128,1024]{1,0:T(8,128)}, f32[128,1024]{1,0:T(8,128)S(1)}, u32[]{:S(2)}) copy-start(f32[128,1024]{1,0:T(8,128)S(1)} %fusion.27) | copy-start | bytes 1572868
  623.7 4.5 copy-start.2
  628.2 0.8 copy-start.4
  685.3 273.9 %all-gather.8.cloned.1.call-start = ((), (), s32[]{:S(2)}) async-start(), calls=%async_computation.6 | async-start | bytes 9437184 | tf_op jit(solution)/shard_map/all_gather | solution.py:50
  959.2 65.7 %slice-start = ((s8[8388608]{0:T(1024)(128)(4,1)}), s8[4194304]{0:T(1024)(128)(4,1)S(1)}, s32[]{:S(2)}) async-start(s8[8388608]{0:T(1024)(128)(4,1)} %bitcast.58), calls=%async_computation.7 | async-start | bytes 8388608
  959.2 65.7 %slice-start.2 = ((s8[16777216]{0:T(1024)(128)(4,1)}), s8[4194304]{0:T(1024)(128)(4,1)S(1)}, s32[]{:S(2)}) async-start(s8[16777216]{0:T(1024)(128)(4,1)} %bitcast.64), calls=%async_computation.9 | async-start | bytes 8388608
  959.2 65.7 %slice-start.3 = ((s8[16777216]{0:T(1024)(128)(4,1)}), s8[4194304]{0:T(1024)(128)(4,1)S(1)}, s32[]{:S(2)}) async-start(s8[16777216]{0:T(1024)(128)(4,1)} %bitcast.64), calls=%async_computation.10 | async-start | bytes 8388608
  968.1 56.8 %slice-start.1 = ((s8[8388608]{0:T(1024)(128)(4,1)}), s8[4194304]{0:T(1024)(128)(4,1)S(1)}, s32[]{:S(2)}) async-start(s8[8388608]{0:T(1024)(128)(4,1)} %bitcast.58), calls=%async_computation.8 | async-start | bytes 8388608
  968.1 56.8 %slice-start.4 = ((s8[16777216]{0:T(1024)(128)(4,1)}), s8[4194304]{0:T(1024)(128)(4,1)S(1)}, s32[]{:S(2)}) async-start(s8[16777216]{0:T(1024)(128)(4,1)} %bitcast.64), calls=%async_computation.11 | async-start | bytes 8388608
  968.1 56.8 %slice-start.5 = ((s8[16777216]{0:T(1024)(128)(4,1)}), s8[4194304]{0:T(1024)(128)(4,1)S(1)}, s32[]{:S(2)}) async-start(s8[16777216]{0:T(1024)(128)(4,1)} %bitcast.64), calls=%async_computation.12 | async-start | bytes 8388608
Sparse Core Ops, SparseCore 0:
  9.5 37.1 all-gather.3
  48.9 227.2 all-gather.5
  336.0 49.5 all-reduce.3
  392.5 78.3 all-reduce.5
  685.4 147.0 reduce-scatter.1
  834.5 124.6 all-gather.7
where the time goes:
time: 1100 us; the launch traced here: 1090 us
  waiting for transfers between devices  626 us (57%)
  matrix products  253 us (23%)
  other arithmetic  132 us (12%)
  blocking collectives  43.3 us (4%)
  local copies, waits for them, and re-layouts  17.1 us (2%)
  between operations  17.1 us (2%)
    all_gather x1, waiting for transfers between devices, body(): lax.all_gather(activations, 'wide', axis=0, tiled=True)  229 us
    reduce_scatter x1, waiting for transfers between devices, body(): lax.psum_scatter(lax.dot_general(buffer, ortho_left, (((0,), (0,)), ((),...  147 us
    all_gather x1, waiting for transfers between devices, body(): right_raw = lax.all_gather(right_share, 'wide', axis=0, tiled=True)  82 us
    another operation x14, other arithmetic, body(): lower_factor = jnp.linalg.cholesky(gram_matrix)  78.6 us
    psum x1, waiting for transfers between devices, body(): gram_matrix = lax.psum(gram_local, 'wide')  78.3 us
    dot_general x1, matrix products, body(): lax.dot_general(ortho_left, right_raw, (((1,), (1,)), ((), ())), precisio...  57.3 us
    dot_general x1, matrix products, body(): lax.dot_general(ortho_left, new_right, (((1,), (1,)), ((), ())), precisio...  56.8 us
    dot_general x1, matrix products, body(): lax.dot_general(buffer, ortho_left, (((0,), (0,)), ((), ())), precision=h...  56.3 us
  transfers between devices with their start and end apart: 6, of which 6 were waited for; matrix products, arithmetic and copies ran while one was open for 0% of the time, Pallas kernels for 0%

commit v1 on v0

v1 whole, which is shorter than its diff:
```python
import math

import jax
import jax.numpy as jnp
from jax import lax
from jax.experimental import pallas as pl
from jax.experimental.pallas import tpu as pltpu
from jax.sharding import PartitionSpec as P


FEEDBACK = 0.05
EPSILON = 1e-06
LANES = 128
CORES = 2
TILE = 512
PAD = 16
BLOCK = 128
UNROLL = 8

HIGH = lax.Precision.HIGH
HIGHEST = lax.Precision.HIGHEST
F32 = jnp.float32
F16 = jnp.float16
BF16 = jnp.bfloat16


def split(x):
    hi = lax.reduce_precision(x, exponent_bits=8, mantissa_bits=7)
    return hi.astype(BF16), (x - hi).astype(BF16)


def dot(a, b, ca, cb, precision=None):
    return lax.dot_general(
        a, b, (((ca,), (cb,)), ((), ())), precision=precision, preferred_element_type=F32
    )


def put(pieces, starts, shape, axis):
    out = jnp.zeros(shape, pieces[0].dtype)
    for piece, start in zip(pieces, starts):
        out = lax.dynamic_update_slice_in_dim(out, piece, start, axis)
    return out


class Ring:
    def __init__(self, name, outer, inner):
        self.name, self.outer, self.inner = name, outer, inner
        index = lax.axis_index(name)
        self.o, self.i = index // inner, lax.rem(index, inner)

    def send(self, x, do, di):
        o, i = self.outer, self.inner
        if do % o == 0 and di % i == 0:
            return x
        pairs = [
            (a * i + b, ((a + do) % o) * i + (b + di) % i) for a in range(o) for b in range(i)
        ]
        return lax.ppermute(x, self.name, pairs)

    def at(self, do, di):
        o, i = self.outer, self.inner
        return lax.rem(self.o + do % o, o) * i + lax.rem(self.i + di % i, i)

    def order(self):
        return [(s, d) for s in range(self.outer) for d in range(self.inner)]

    def blocks(self, x):
        found = []
        for s, d in self.order():
            found.append(self.send(x, s, d))
        return jnp.concatenate(found, axis=0)

    def gather(self, x, spread=False):
        found, held, aside = {}, x, {}
        for s in range(self.outer):
            held = self.send(held, 1, 0) if s else held
            found[s, 0] = held
            for d in range(1, self.inner):
                if spread and s == self.outer - 1:
                    half = x.shape[1] // 2
                    near = self.send(held[:, :half], 0, d)
                    far = self.send(aside[d][:, half:], 1, 0)
                    found[s, d] = jnp.concatenate([near, far], axis=1)
                else:
                    aside[d] = found[s, d] = self.send(held, 0, d)
        return [found[key] for key in self.order()]

    def scatter_sum(self, piece):
        total = None
        for j in range(self.outer):
            back = -1 - j
            mine = piece(self.at(back, 0))
            for d in range(1, self.inner):
                got = self.send(piece(self.at(back, d)), 0, d)
                mine = mine + got
            if total is not None:
                total = self.send(total, 1, 0)
            total = mine if total is None else total + mine
        return total

    def total(self, x):
        count, step = self.outer * self.inner, 1
        while step < count:
            got = lax.ppermute(x, self.name, [(k, k ^ step) for k in range(count)])
            x = x + got
            step *= 2
        return x


def narrow_sum(ring, x, width):
    cut = lambda index: lax.dynamic_slice_in_dim(x, index * width, width, 1)
    keep = [cut(ring.at(s, 0)) for s in range(ring.outer)]
    give = [cut(ring.at(s, 1)) for s in range(ring.outer)]
    got = ring.send(jnp.concatenate(give, axis=1), 0, 1)
    kept = [k + got[:, s * width : (s + 1) * width] for s, k in enumerate(keep)]
    total = kept[0]
    for s in range(1, ring.outer):
        got = ring.send(kept[s], s, 0)
        total = total + got
    return total


def narrow_collect(ring, x, axis):
    size = x.shape[axis]
    shape = list(x.shape)
    shape[axis] = size * ring.outer * ring.inner
    mine = []
    for s in range(ring.outer):
        mine.append(ring.send(x, s, 0))
    other = ring.send(jnp.concatenate(mine, axis=axis), 0, 1)
    pieces, starts = [], []
    for s in range(ring.outer):
        pieces += [mine[s], lax.slice_in_dim(other, s * size, (s + 1) * size, axis=axis)]
        starts += [ring.at(-s, 0) * size, ring.at(-s, 1) * size]
    return put(pieces, starts, shape, axis)


def buffer_kernel(count, grads, left_hi, left_lo, momentum, *refs):
    acts, (buffer_out, product_out) = refs[:count], refs[-2:]
    rows = jnp.concatenate([a[...] for a in acts], axis=0)
    buffer = momentum[...] + jnp.dot(grads[...], rows, preferred_element_type=F32)
    buffer_out[...] = buffer
    hi = buffer.astype(BF16)
    lo = (buffer - hi.astype(F32)).astype(BF16)
    product = jnp.dot(left_hi[...], hi, preferred_element_type=F32)
    product += jnp.dot(left_hi[...], lo, preferred_element_type=F32)
    product += jnp.dot(left_lo[...], hi, preferred_element_type=F32)
    product_out[...] = product


def buffer_call(half, grads, left_hi, left_lo, momentum, acts, buffer):
    rows, columns = momentum.shape
    rank = left_hi.shape[0]
    width = acts[0].shape[1]
    tile = min(TILE, width)
    first = half * width // tile
    resident = lambda a: pl.BlockSpec(a.shape, lambda j: (0, 0), pipeline_mode=pl.Buffered(1))
    moving = lambda r: pl.BlockSpec((r, tile), lambda j: (0, j))
    placed = pl.BlockSpec((rows, tile), lambda j: (0, first + j))
    in_specs = [resident(grads), resident(left_hi), resident(left_lo), placed]
    in_specs += [moving(a.shape[0]) for a in acts]
    args = [grads, left_hi, left_lo, momentum, *acts]
    aliases = {}
    if buffer is not None:
        aliases = {len(args): 0}
        in_specs.append(pl.BlockSpec(memory_space=pl.ANY))
        args.append(buffer)
    tokens = grads.shape[1]
    flops = 2 * rows * width * (tokens + 3 * rank)
    count = len(acts)
    return pl.pallas_call(
        lambda *refs: buffer_kernel(count, *refs),
        grid=(width // tile,),
        in_specs=in_specs,
        out_specs=[placed, moving(rank)],
        out_shape=[
            jax.ShapeDtypeStruct((rows, columns), F32),
            jax.ShapeDtypeStruct((rank, width), F32),
        ],
        input_output_aliases=aliases,
        compiler_params=pltpu.CompilerParams(
            dimension_semantics=("arbitrary",), vmem_limit_bytes=56 << 20
        ),
        cost_estimate=pl.CostEstimate(
            flops=flops, transcendentals=0, bytes_accessed=width * (8 * rows + 2 * tokens + 4 * rank)
        ),
        name="buffer_product",
    )(*args)


def feedback_kernel(places, ortho, buffer, *refs):
    del places
    rights, (out, squares) = refs[:-2], refs[-2:]
    for k, right in enumerate(rights):

        @pl.when(pl.program_id(0) == k)
        def _(right=right):
            product = dot(ortho[...], right[...].astype(BF16), 1, 1)
            out[...] = buffer[...] - product
            square = jnp.sum(right[...] * right[...], axis=0, keepdims=True)
            squares[...] = square if k == 0 else squares[...] + square


def feedback_call(ortho, buffer, rights, places):
    rows = buffer.shape[0]
    strip, rank = rights[0].shape
    whole = lambda a: pl.BlockSpec(a.shape, lambda k, p: (0, 0), pipeline_mode=pl.Buffered(1))
    placed = pl.BlockSpec((rows, strip), lambda k, p: (0, p[k]))
    count = len(rights)
    return pl.pallas_call(
        feedback_kernel,
        grid_spec=pltpu.PrefetchScalarGridSpec(
            num_scalar_prefetch=1,
            grid=(count,),
            in_specs=[whole(ortho), placed] + [whole(r) for r in rights],
            out_specs=[placed, pl.BlockSpec((1, rank), lambda k, p: (0, 0))],
        ),
        out_shape=[
            jax.ShapeDtypeStruct(buffer.shape, F32),
            jax.ShapeDtypeStruct((1, rank), F32),
        ],
        input_output_aliases={2: 0},
        compiler_params=pltpu.CompilerParams(
            dimension_semantics=("arbitrary",), vmem_limit_bytes=32 << 20
        ),
        cost_estimate=pl.CostEstimate(
            flops=2 * rows * strip * rank * count,
            transcendentals=0,
            bytes_accessed=8 * rows * strip * count,
        ),
        name="feedback",
    )(places, ortho, buffer, *rights)


def update_kernel(q_hi, q_lo, inv_norm, raw, update, right):
    value = raw[...]
    right[...] = value * inv_norm[...]
    hi = value.astype(BF16)
    lo = (value - hi.astype(F32)).astype(BF16)
    product = dot(q_hi[...], hi, 1, 1) + dot(q_hi[...], lo, 1, 1) + dot(q_lo[...], hi, 1, 1)
    update[...] = product.astype(BF16)


def update_call(q_hi, q_lo, inv_norm, raw):
    rows, rank = q_hi.shape
    columns = raw.shape[0]
    tile = min(TILE, columns)
    whole = lambda a: pl.BlockSpec(a.shape, lambda j: (0, 0), pipeline_mode=pl.Buffered(1))
    tall = pl.BlockSpec((tile, rank), lambda j: (j, 0))
    return pl.pallas_call(
        update_kernel,
        grid=(columns // tile,),
        in_specs=[whole(q_hi), whole(q_lo), whole(inv_norm), tall],
        out_specs=[pl.BlockSpec((rows, tile), lambda j: (0, j)), tall],
        out_shape=[
            jax.ShapeDtypeStruct((rows, columns), BF16),
            jax.ShapeDtypeStruct((columns, rank), F32),
        ],
        compiler_params=pltpu.CompilerParams(
            dimension_semantics=("arbitrary",), vmem_limit_bytes=40 << 20
        ),
        cost_estimate=pl.CostEstimate(
            flops=6 * rows * columns * rank,
            transcendentals=0,
            bytes_accessed=columns * (2 * rows + 8 * rank),
        ),
        name="update",
    )(q_hi, q_lo, inv_norm, raw)


def eliminate(block, unroll):
    size = block.shape[0]
    rows = lax.broadcasted_iota(jnp.int32, (size, size), 0)
    lanes = lax.broadcasted_iota(jnp.int32, (size, size), 1)
    row = lax.broadcasted_iota(jnp.int32, (size, 1), 0)

    def lane(j, work):
        return jnp.sum(jnp.where(lanes == j, work, 0.0), axis=1, keepdims=True)

    def entry(j, column):
        return jnp.sum(jnp.where(row == j, column, 0.0), axis=0, keepdims=True)

    def step(j, carry):
        work, inverse, pivots, column = carry
        here = rows == j
        ahead = lane(j + 1, work)
        across = jnp.sum(jnp.where(here, work, 0.0), axis=0, keepdims=True)
        beside = jnp.sum(jnp.where(here, inverse, 0.0), axis=0, keepdims=True)
        pivot = entry(j, column)
        factor = jnp.where(row > j, column / pivot, 0.0)
        work = work - factor * across
        inverse = inverse - factor * beside
        ahead = ahead - factor * entry(j + 1, column)
        return work, inverse, jnp.where(row == j, pivot, pivots), ahead

    start = (block, (rows == lanes).astype(F32), jnp.ones((size, 1), F32), lane(0, block))
    _, inverse, pivots, _ = lax.fori_loop(0, size, step, start, unroll=unroll)
    return inverse * (1.0 / jnp.sqrt(pivots))


def inverse_kernel(first, size, *refs):
    work_in, inverse_in = refs[0], refs[-3]
    work, inverse = refs[-2:]
    total = work.shape[0]
    last = first + size
    work[...] = work_in[...]
    if first:
        inverse[...] = inverse_in[...]
    else:
        rows = lax.broadcasted_iota(jnp.int32, (total, total), 0)
        lanes = lax.broadcasted_iota(jnp.int32, (total, total), 1)
        inverse[...] = (rows == lanes).astype(F32)
    block = eliminate(work[first:last, first:last], UNROLL)
    strip = dot(block, inverse[first:last, :], 1, 0, HIGHEST)
    inverse[first:last, :] = strip
    if last < total:
        panel = dot(work[last:, first:last], block, 1, 1, HIGHEST)
        inverse[last:, :] = inverse[last:, :] - dot(panel, strip, 1, 0, HIGHEST)
        work[last:, last:] = work[last:, last:] - dot(panel, panel, 1, 1, HIGHEST)


def cholesky_inverse(gram):
    total = gram.shape[0]
    size = min(BLOCK, total)
    state = [gram]
    for first in range(0, total, size):
        state = pl.pallas_call(
            lambda *refs, first=first: inverse_kernel(first, size, *refs),
            out_shape=[jax.ShapeDtypeStruct(gram.shape, F32)] * 2,
            compiler_params=pltpu.CompilerParams(vmem_limit_bytes=24 << 20),
            name="cholesky_inverse",
        )(*state)
    return state[1]


def body(outer, dout, din, activations, grad_out, momentum, right_factor):
    wide = Ring("wide", outer, lax.axis_size("wide") // outer)
    narrow = Ring("narrow", lax.axis_size("narrow") // CORES, CORES)
    rank = right_factor.shape[1]
    tokens, columns = activations.shape
    members, seats = wide.outer * wide.inner, narrow.outer * narrow.inner
    halves = 2 if columns % (2 * members * LANES) == 0 else 1
    width = columns // halves
    strip = width // members
    quarter = rank // seats

    v_hi, v_lo = split(right_factor)
    av = dot(activations, v_hi, 1, 0) + dot(activations, v_lo, 1, 0)
    av = narrow_sum(narrow, av, quarter)
    av_hi, av_lo = split(wide.blocks(av))

    acts = [
        wide.gather(activations[:, h * width : (h + 1) * width], spread=wide.inner == 2)
        for h in range(halves)
    ]
    all_grads = narrow_collect(narrow, grad_out, 0)
    grads = jnp.concatenate(
        [
            lax.dynamic_slice_in_dim(all_grads, wide.at(-s, -d) * tokens, tokens, 0)
            for s, d in wide.order()
        ],
        axis=0,
    ).T

    mv = dot(momentum, right_factor, 1, 0, HIGH)
    mv = narrow_sum(narrow, mv, quarter)
    left_part = mv + (dot(grads, av_hi, 1, 0) + dot(grads, av_lo, 1, 0))
    left = narrow_collect(narrow, left_part, 1)

    gram_part = dot(left_part, left, 0, 0, HIGHEST)
    gram = narrow_collect(narrow, wide.total(gram_part), 0)
    inverse = cholesky_inverse(gram)
    ortho = dot(left, inverse, 1, 1, HIGH)

    left_hi, left_lo = split(left.T)
    buffer, shares = None, []
    for h in range(halves):
        buffer, product = buffer_call(h, grads, left_hi, left_lo, momentum, acts[h], buffer)
        shares.append(
            wide.scatter_sum(
                lambda index, p=product: lax.dynamic_slice_in_dim(p, index * strip, strip, 1),
            )
        )

    share = dot(jnp.concatenate(shares, axis=1), inverse, 0, 1, HIGHEST)
    own = jnp.sum(share * share, axis=0)
    size = jnp.sqrt(own / share.shape[0])
    exponent = jnp.floor(jnp.log2(jnp.where(size > 0, size, 1.0)))
    sent = jnp.concatenate(
        [
            (share * jnp.exp2(-exponent)[None, :]).astype(F16),
            jnp.broadcast_to(exponent.astype(F16)[None, :], (PAD, rank)),
        ],
        axis=0,
    )
    feedback_left = (FEEDBACK * ortho).astype(BF16)
    gathered = dict(zip(wide.order(), wide.gather(sent, spread=wide.inner == 2)))
    pieces, starts, squares = [], [], []
    for s in range(wide.outer):
        rights, places = [], []
        for d in range(wide.inner):
            got = gathered[s, d]
            value = got[:-PAD].astype(F32) * jnp.exp2(got[-PAD : -PAD + 1].astype(F32))
            value = lax.optimization_barrier(value)
            for h in range(halves):
                place = h * members + wide.at(-s, -d)
                rights.append(value[h * strip : (h + 1) * strip])
                places.append(place)
                starts.append(place * strip)
        pieces += rights
        buffer, square = feedback_call(feedback_left, buffer, rights, jnp.stack(places))
        squares.append(square)
    raw = put(pieces, starts, (columns, rank), 0)
    col_squares = narrow.total(sum(squares))
    inv_norm = 1.0 / (jnp.sqrt(col_squares) + EPSILON)
    q_hi, q_lo = split(ortho * (math.sqrt(dout * din / rank) * inv_norm))
    update, new_right = update_call(q_hi, q_lo, inv_norm, raw)
    return buffer, new_right, update


def solution(mesh):
    members = mesh.shape["wide"]
    outer = 1 << -(-(members.bit_length() - 1) // 2)

    def local(dout, din, *arrays):
        return body(outer, dout, din, *arrays)

    def whole(activations, grad_out, momentum, right_factor):
        dout, din = momentum.shape
        return jax.shard_map(
            lambda *arrays: local(dout, din, *arrays),
            mesh=mesh,
            in_specs=(P("wide", "narrow"), P("narrow", "wide"), P("wide", "narrow"), P("narrow", None)),
            out_specs=(P("wide", "narrow"), P("narrow", None), P("wide", "narrow")),
            check_vma=False,
        )(activations, grad_out, momentum, right_factor)

    return whole
```

time: 1100 us -> 565 us (0.51)
  waiting for transfers between devices: 626 us -> 277 us
  matrix products: 253 us -> 38.9 us
  Pallas kernels: 0 us -> 128 us
  other arithmetic: 132 us -> 29.3 us
  starting transfers between devices: 0.41 us -> 57.8 us
  blocking collectives: 43.3 us -> 0 us
  between operations: 17.1 us -> 1.87 us
    all_gather x3 -> x0, waiting for transfers between devices: 349 us -> none  [the longest x1 229 us: body(): lax.all_gather(activations, 'wide', axis=0, tiled=True)]
    ppermute x0 -> x60, waiting for transfers between devices: none -> 277 us  [the longest x55 234 us: send(): return lax.ppermute(x, self.name, pairs)]
    dot_general x6 -> x8, matrix products: 237 us -> 38.9 us  [dot(): lax.dot_general(a, b, (((ca,), (cb,)), ((), ())), precision=precision, pr...]
    reduce_scatter x1 -> x0, waiting for transfers between devices: 147 us -> none  [body(): lax.psum_scatter(lax.dot_general(buffer, ortho_left, (((0,), (0,)), ((),...]
    pallas_call x0 -> x11, Pallas kernels: none -> 128 us  [the longest x4 43.5 us: cholesky_inverse(): pl.pallas_call(lambda *refs, first=first: inverse_kernel(first, size, *re...]
    psum x2 -> x0, waiting for transfers between devices: 128 us -> none  [the longest x1 78.3 us: body(): gram_matrix = lax.psum(gram_local, 'wide')]
    another operation x17 -> x4, other arithmetic: 120 us -> 0.31 us  [body(): jnp.stack(places)]
    ppermute x0 -> x60, starting transfers between devices: none -> 57.8 us  [the longest x55 55.1 us: send(): return lax.ppermute(x, self.name, pairs)]
  transfers between devices with their start and end apart: 6 -> 60, of which waited for: 6 -> 29; matrix products, arithmetic and copies ran while one was open for 0% -> 15% of each run, Pallas kernels for 0% -> 19%
where the time goes in v1:
time: 565 us; the launch traced here: 555 us
  waiting for transfers between devices  277 us (49%)
  Pallas kernels  128 us (23%)
  starting transfers between devices  57.8 us (10%)
  matrix products  38.9 us (7%)
  other arithmetic  29.3 us (5%)
  local copies, waits for them, and re-layouts  22 us (4%)
    ppermute x55, waiting for transfers between devices, send(): return lax.ppermute(x, self.name, pairs)  234 us
    ppermute x55, starting transfers between devices, send(): return lax.ppermute(x, self.name, pairs)  55.1 us
    pallas_call x4, Pallas kernels, cholesky_inverse(): pl.pallas_call(lambda *refs, first=first: inverse_kernel(first, size, *re...  43.5 us
    pallas_call x2, Pallas kernels, buffer_call(): pl.pallas_call(lambda *refs: buffer_kernel(count, *refs), grid=(width //...  43.1 us
    ppermute x5, waiting for transfers between devices, total(): got = lax.ppermute(x, self.name, [(k, k ^ step) for k in range(count)])  43.1 us
    dot_general x8, matrix products, dot(): lax.dot_general(a, b, (((ca,), (cb,)), ((), ())), precision=precision, pr...  38.9 us
    pallas_call x4, Pallas kernels, feedback_call(): pl.pallas_call(feedback_kernel, grid_spec=pltpu.PrefetchScalarGridSpec(nu...  25.6 us
    pallas_call x1, Pallas kernels, update_call(): pl.pallas_call(update_kernel, grid=(columns // tile,), in_specs=[whole(q_...  15.8 us
  transfers between devices with their start and end apart: 60, of which 29 were waited for; matrix products, arithmetic and copies ran while one was open for 15% of the time, Pallas kernels for 19%

profile of v1, /device:TPU:0, one launch (start us, length us, event | category | flops | bytes accessed | tf_op | source)
XLA Modules:
  0.0 555.3 jit_solution(17441884644582867686)
XLA Ops:
  2.2 3.1 collective-permute-start.2
  5.2 5.3 fusion.3
  20.9 8.4 %collective-permute-done.2 = bf16[512,1024]{0,1:T(8,128)(2,1)} collective-permute-done((bf16[512,1024]{0,1:T(8,128)(2,1)S(1)}, bf16[512,1024]{0,1:T(8,128)(2,1)}, u32[]{:S(2)}, u32[]{:S(2)}) %collective-permute-start.2) | collective-permute-done | bytes 1048608 | tf_op jit(solution)/shard_map/ppermute | solution.py:58
  29.3 2.8 pad_maximum_fusion
  32.1 19.3 %fusion.45 = f32[1024,512]{0,1:T(8,128)} fusion(f32[1024,4096]{1,0:T(8,128)} %refs_3_.3, f32[4096,512]{1,0:T(8,128)} %param.7), kind=kOutput, calls=%fused_computation.151 | convolution fusion | flops 12884901888 | bytes 27262976 | tf_op jit(solution)/shard_map/dot_general | solution.py:33
  59.5 2.8 collective-permute-start.8
  63.3 5.6 %collective-permute-done.7 = f32[256,128]{1,0:T(8,128)S(1)} collective-permute-done((f32[256,128]{1,0:T(8,128)}, f32[256,128]{1,0:T(8,128)S(1)}, u32[]{:S(2)}, u32[]{:S(2)}) %collective-permute-start.7) | collective-permute-done | bytes 131104 | tf_op jit(solution)/shard_map/ppermute | solution.py:58
  68.9 3.5 collective-permute-done.8
  73.8 6.7 %collective-permute-done.9 = f32[256,128]{1,0:T(8,128)S(1)} collective-permute-done((f32[256,128]{1,0:T(8,128)}, f32[256,128]{1,0:T(8,128)S(1)}, u32[]{:S(2)}, u32[]{:S(2)}) %collective-permute-start.9) | collective-permute-done | bytes 131104 | tf_op jit(solution)/shard_map/ppermute | solution.py:58
  80.5 3.0 collective-permute-start.31
  84.2 50.7 %collective-permute-done.10 = f32[256,128]{1,0:T(8,128)S(1)} collective-permute-done((f32[256,128]{1,0:T(8,128)}, f32[256,128]{1,0:T(8,128)S(1)}, u32[]{:S(2)}, u32[]{:S(2)}) %collective-permute-start.10) | collective-permute-done | bytes 131104 | tf_op jit(solution)/shard_map/ppermute | solution.py:58
  134.9 5.6 %collective-permute-done.11 = f32[256,128]{1,0:T(8,128)S(1)} collective-permute-done((f32[256,128]{1,0:T(8,128)}, f32[256,128]{1,0:T(8,128)S(1)}, u32[]{:S(2)}, u32[]{:S(2)}) %collective-permute-start.11) | collective-permute-done | bytes 131104 | tf_op jit(solution)/shard_map/ppermute | solution.py:58
  140.5 2.7 collective-permute-start.12
  143.3 3.3 collective-permute-done.12
  161.5 10.1 %collective-permute-done.13 = f32[1024,128]{0,1:T(8,128)S(1)} collective-permute-done((f32[1024,128]{0,1:T(8,128)S(1)}, f32[1024,128]{0,1:T(8,128)S(1)}, u32[]{:S(2)}, u32[]{:S(2)}) %collective-permute-start.13) | collective-permute-done | bytes 524320 | tf_op jit(solution)/shard_map/ppermute | solution.py:58
  171.8 3.9 collective-permute-done.33.refs_10_
  177.1 21.0 %collective-permute-done.25.refs_10_ = bf16[256,2048]{1,0:T(8,128)(2,1)S(1)} collective-permute-done((bf16[256,2048]{1,0:T(8,128)(2,1)S(1)}, bf16[256,2048]{1,0:T(8,128)(2,1)S(1)}, u32[]{:S(2)}, u32[]{:S(2)}) %collective-permute-start.25) | collective-permute-done | bytes 1048608 | tf_op jit(solution)/shard_map/ppermute | solution.py:58
  199.6 8.0 %collective-permute-done.34 = bf16[256,1024]{1,0:T(8,128)(2,1)S(1)} collective-permute-done((bf16[256,1024]{1,0:T(8,128)(2,1)S(1)}, bf16[256,1024]{1,0:T(8,128)(2,1)S(1)}, u32[]{:S(2)}, u32[]{:S(2)}) %collective-permute-start.34) | collective-permute-done | bytes 524320 | tf_op jit(solution)/shard_map/ppermute | solution.py:58
  211.7 7.2 %collective-permute-done.26 = bf16[256,1024]{1,0:T(8,128)(2,1)S(1)} collective-permute-done((bf16[256,1024]{1,0:T(8,128)(2,1)S(1)}, bf16[256,1024]{1,0:T(8,128)(2,1)S(1)}, u32[]{:S(2)}, u32[]{:S(2)}) %collective-permute-start.26) | collective-permute-done | bytes 524320 | tf_op jit(solution)/shard_map/ppermute | solution.py:58
  223.9 17.4 %collective-permute-done.28.refs_5_ = bf16[256,2048]{1,0:T(8,128)(2,1)S(1)} collective-permute-done((bf16[256,2048]{1,0:T(8,128)(2,1)}, bf16[256,2048]{1,0:T(8,128)(2,1)S(1)}, u32[]{:S(2)}, u32[]{:S(2)}) %collective-permute-start.28) | collective-permute-done | bytes 1048608 | tf_op jit(solution)/shard_map/ppermute | solution.py:58
  241.3 45.0 %collective-permute-done.30.refs_7_ = bf16[256,2048]{1,0:T(8,128)(2,1)} collective-permute-done((bf16[256,2048]{1,0:T(8,128)(2,1)}, bf16[256,2048]{1,0:T(8,128)(2,1)}, u32[]{:S(2)}, u32[]{:S(2)}) %collective-permute-start.30) | collective-permute-done | bytes 1048608 | tf_op jit(solution)/shard_map/ppermute | solution.py:58
  286.3 21.6 %buffer_product.2 = (f32[1024,4096]{1,0:T(8,128)}, f32[512,2048]{1,0:T(8,128)}) custom-call(bf16[1024,2048]{1,0:T(8,128)(2,1)} %bitcast.43, bf16[512,1024]{1,0:T(8,128)(2,1)} %get-tuple-element.70.refs_1_, bf16[512,1024]{1,0:T(8,128)(2,1)} %get-tuple-element.69.refs_2_, f32[1024,4096]{1,0:T(8,128)} %refs_3_.3, bf16[256,2048]{1,0:T(8,128)(2,1)} %get-tuple-element.67.refs_4_, ...), custom_call_target="tpu_custom_call" | custom-call | flops 15032385536 | bytes 29360128 | tf_op jit(solution)/shard_map/buffer_product/pallas_call | solution.py:171
  307.9 2.9 constant_dynamic-slice_fusion.4
  316.2 21.6 %buffer_product.3 = (f32[1024,4096]{1,0:T(8,128)}, f32[512,2048]{1,0:T(8,128)}) custom-call(bf16[1024,2048]{1,0:T(8,128)(2,1)} %bitcast.44, bf16[512,1024]{1,0:T(8,128)(2,1)} %get-tuple-element.70.refs_1_, bf16[512,1024]{1,0:T(8,128)(2,1)} %get-tuple-element.69.refs_2_, f32[1024,4096]{1,0:T(8,128)} %refs_3_.3, ...), custom_call_target="tpu_custom_call", output_to_operand_aliasing={{0}: (12, {})} | custom-call | flops 15032385536 | bytes 29360128 | tf_op jit(solution)/shard_map/buffer_product/pallas_call | solution.py:171
  337.7 2.9 constant_dynamic-slice_fusion
  348.0 9.2 %collective-permute-done.16 = f32[128,512]{1,0:T(8,128)S(1)} collective-permute-done((f32[128,512]{1,0:T(8,128)S(1)}, f32[128,512]{1,0:T(8,128)S(1)}, u32[]{:S(2)}, u32[]{:S(2)}) %collective-permute-start.16) | collective-permute-done | bytes 262176 | tf_op jit(solution)/shard_map/ppermute | solution.py:104
  359.9 30.0 %collective-permute-done.17 = f32[128,512]{1,0:T(8,128)S(1)} collective-permute-done((f32[128,512]{1,0:T(8,128)S(1)}, f32[128,512]{1,0:T(8,128)S(1)}, u32[]{:S(2)}, u32[]{:S(2)}) %collective-permute-start.17) | collective-permute-done | bytes 262176 | tf_op jit(solution)/shard_map/ppermute | solution.py:104
  395.5 2.3 add_add_fusion.5
  397.8 2.3 add_add_fusion.2
  404.1 5.0 collective-permute-done.39
  410.7 4.1 collective-permute-done.46
  416.6 11.6 %cholesky_inverse.4 = (f32[512,512]{1,0:T(8,128)S(1)}, f32[512,512]{1,0:T(8,128)S(1)}) custom-call(f32[512,512]{1,0:T(8,128)S(1)} %slice_dynamic-update-slice_fusion.4.refs_0_), custom_call_target="tpu_custom_call" | custom-call | tf_op jit(solution)/shard_map/cholesky_inverse/pallas_call | solution.py:327
  428.2 11.0 %cholesky_inverse.5 = (f32[512,512]{1,0:T(8,128)S(1)}, f32[512,512]{1,0:T(8,128)S(1)}) custom-call(f32[512,512]{1,0:T(8,128)S(1)} %get-tuple-element.24.refs_0_, f32[512,512]{1,0:T(8,128)S(1)} %get-tuple-element.25.refs_1_), custom_call_target="tpu_custom_call" | custom-call | tf_op jit(solution)/shard_map/cholesky_inverse/pallas_call | solution.py:327
  439.2 10.6 %cholesky_inverse.6 = (f32[512,512]{1,0:T(8,128)S(1)}, f32[512,512]{1,0:T(8,128)S(1)}) custom-call(f32[512,512]{1,0:T(8,128)S(1)} %get-tuple-element.26.refs_0_, f32[512,512]{1,0:T(8,128)S(1)} %get-tuple-element.27.refs_1_), custom_call_target="tpu_custom_call" | custom-call | tf_op jit(solution)/shard_map/cholesky_inverse/pallas_call | solution.py:327
  449.8 10.3 %cholesky_inverse.7 = (f32[512,512]{1,0:T(8,128)}, f32[512,512]{1,0:T(8,128)S(1)}) custom-call(f32[512,512]{1,0:T(8,128)S(1)} %get-tuple-element.28.refs_0_, f32[512,512]{1,0:T(8,128)S(1)} %get-tuple-element.29.refs_1_), custom_call_target="tpu_custom_call" | custom-call | tf_op jit(solution)/shard_map/cholesky_inverse/pallas_call | solution.py:327
  462.5 3.5 multiply_reduce_fusion
  467.2 3.5 multiply_convert_fusion
  472.0 5.0 collective-permute-done.50
  477.4 5.5 collective-permute-done.51
  484.3 6.3 %feedback.4 = (f32[1024,4096]{1,0:T(8,128)}, f32[1,512]{1,0:T(1,128)S(1)}) custom-call(s32[4]{0:T(128)S(1)} %pad_add_fusion.3.places, bf16[1024,512]{1,0:T(8,128)(2,1)S(1)} %get-tuple-element.100.ortho, f32[1024,4096]{1,0:T(8,128)} %get-tuple-element.32.buffer, f32[256,512]{1,0:T(8,128)S(1)} %get-tuple-element.96.refs_0_, ...), custom_call_target="tpu_custom_call", output_to_operand_aliasing={{0}: (2, {})} | custom-call | flops 1073741824 | bytes 8388608 | tf_op jit(solution)/shard_map/feedback/pallas_call | solution.py:210
  492.8 9.0 %collective-permute-done.53 = f16[528,512]{1,0:T(8,128)(2,1)S(1)} collective-permute-done((f16[528,512]{1,0:T(8,128)(2,1)S(1)}, f16[528,512]{1,0:T(8,128)(2,1)S(1)}, u32[]{:S(2)}, u32[]{:S(2)}) %collective-permute-start.53) | collective-permute-done | bytes 540704 | tf_op jit(solution)/shard_map/ppermute | solution.py:58
  504.4 6.5 %feedback.5 = (f32[1024,4096]{1,0:T(8,128)}, f32[1,512]{1,0:T(1,128)S(1)}) custom-call(s32[4]{0:T(128)S(1)} %pad_add_fusion.2.places, bf16[1024,512]{1,0:T(8,128)(2,1)S(1)} %get-tuple-element.100.ortho, f32[1024,4096]{1,0:T(8,128)} %get-tuple-element.35.buffer, f32[256,512]{1,0:T(8,128)S(1)} %get-tuple-element.90.refs_0_, ...), custom_call_target="tpu_custom_call", output_to_operand_aliasing={{0}: (2, {})} | custom-call | flops 1073741824 | bytes 8388608 | tf_op jit(solution)/shard_map/feedback/pallas_call | solution.py:210
  511.1 3.9 collective-permute-done.55
  516.1 4.0 collective-permute-start.57
  520.9 6.3 %feedback.6 = (f32[1024,4096]{1,0:T(8,128)}, f32[1,512]{1,0:T(1,128)S(1)}) custom-call(s32[4]{0:T(128)S(1)} %pad_add_fusion.1.places, bf16[1024,512]{1,0:T(8,128)(2,1)S(1)} %get-tuple-element.100.ortho, f32[1024,4096]{1,0:T(8,128)} %get-tuple-element.36.buffer, f32[256,512]{1,0:T(8,128)S(1)} %get-tuple-element.84.refs_0_, ...), custom_call_target="tpu_custom_call", output_to_operand_aliasing={{0}: (2, {})} | custom-call | flops 1073741824 | bytes 8388608 | tf_op jit(solution)/shard_map/feedback/pallas_call | solution.py:210
  527.7 6.3 %feedback.7 = (f32[1024,4096]{1,0:T(8,128)}, f32[1,512]{1,0:T(1,128)S(1)}) custom-call(s32[4]{0:T(128)S(1)} %pad_add_fusion.places, bf16[1024,512]{1,0:T(8,128)(2,1)S(1)} %get-tuple-element.100.ortho, f32[1024,4096]{1,0:T(8,128)} %get-tuple-element.37.buffer, f32[256,512]{1,0:T(8,128)S(1)} %get-tuple-element.78.refs_0_, ...), custom_call_target="tpu_custom_call", output_to_operand_aliasing={{0}: (2, {})} | custom-call | flops 1073741824 | bytes 8388608 | tf_op jit(solution)/shard_map/feedback/pallas_call | solution.py:210
  536.3 2.6 collective-permute-done.59
  539.3 15.8 %update.1 = (bf16[1024,4096]{1,0:T(8,128)(2,1)}, f32[4096,512]{1,0:T(8,128)}) custom-call(bf16[1024,512]{1,0:T(8,128)(2,1)S(1)} %get-tuple-element.66.q_hi, bf16[1024,512]{1,0:T(8,128)(2,1)S(1)} %get-tuple-element.65.q_lo, f32[1,512]{1,0:T(1,128)S(1)} %get-tuple-element.46.inv_norm, f32[4096,512]{1,0:T(8,128)S(1)} %get-tuple-element.73.raw), custom_call_target="tpu_custom_call" | custom-call | flops 12884901888 | bytes 25165824 | tf_op jit(solution)/shard_map/update/pallas_call | solution.py:250
  (228 shorter events, 94.3 us)
Async XLA Ops:
  2.2 27.2 %collective-permute-start.2 = (bf16[512,1024]{0,1:T(8,128)(2,1)S(1)}, bf16[512,1024]{0,1:T(8,128)(2,1)}, u32[]{:S(2)}, u32[]{:S(2)}) collective-permute-start(bf16[512,1024]{0,1:T(8,128)(2,1)S(1)} %copy.12), channel_id=1, source_target_pairs={{0,2},{1,3},{2,0},{3,1},{4,6},{5,7},{6,4},{7,5},{8,10},{9,11},{10,... | collective-permute-start | bytes 3145736 | tf_op jit(solution)/shard_map/ppermute | solution.py:58
  15.4 65.1 %collective-permute-start.29 = (bf16[256,2048]{1,0:T(8,128)(2,1)}, bf16[256,2048]{1,0:T(8,128)(2,1)}, u32[]{:S(2)}, u32[]{:S(2)}) collective-permute-start(bf16[256,2048]{1,0:T(8,128)(2,1)} %get-tuple-element.67.refs_4_), channel_id=1, source_target_pairs={{0,8},{4,12},{8,16},{12,20},{16,24},{20,28},{24,0},{28,4},{1,9},{5... | collective-permute-start | bytes 3145736 | tf_op jit(solution)/shard_map/ppermute | solution.py:58
  17.3 66.2 %collective-permute-start.21 = (bf16[256,2048]{1,0:T(8,128)(2,1)}, bf16[256,2048]{1,0:T(8,128)(2,1)}, u32[]{:S(2)}, u32[]{:S(2)}) collective-permute-start(bf16[256,2048]{1,0:T(8,128)(2,1)} %get-tuple-element.68.refs_4_), channel_id=1, source_target_pairs={{0,8},{4,12},{8,16},{12,20},{16,24},{20,28},{24,0},{28,4},{1,9},{5... | collective-permute-start | bytes 3145736 | tf_op jit(solution)/shard_map/ppermute | solution.py:58
  19.9 31.6 %collective-permute-start.5 = (f32[256,128]{1,0:T(8,128)S(1)}, f32[256,128]{1,0:T(8,128)S(1)}, u32[]{:S(2)}, u32[]{:S(2)}) collective-permute-start(f32[256,128]{1,0:T(8,128)S(1)} %slice_add_fusion.2), channel_id=1, source_target_pairs={{0,2},{1,3},{2,0},{3,1},{4,6},{5,7},{6,4},{7,5},{8,10},{9,11},{10,... | collective-permute-start | bytes 393224 | tf_op jit(solution)/shard_map/ppermute | solution.py:58
  32.1 117.6 %collective-permute-start.3 = (bf16[1024,1024]{0,1:T(8,128)(2,1)}, bf16[1024,1024]{0,1:T(8,128)(2,1)}, u32[]{:S(2)}, u32[]{:S(2)}) collective-permute-start(bf16[1024,1024]{0,1:T(8,128)(2,1)} %pad_maximum_fusion), channel_id=1, source_target_pairs={{0,1},{1,0},{2,3},{3,2},{4,5},{5,4},{6,7},{7,6},{8,9},{9,8},{10,11... | collective-permute-start | bytes 6291464 | tf_op jit(solution)/shard_map/ppermute | solution.py:58
  56.4 12.5 %collective-permute-start.7 = (f32[256,128]{1,0:T(8,128)}, f32[256,128]{1,0:T(8,128)S(1)}, u32[]{:S(2)}, u32[]{:S(2)}) collective-permute-start(f32[256,128]{1,0:T(8,128)} %get-tuple-element.56), channel_id=1, source_target_pairs={{0,8},{4,12},{8,16},{12,20},{16,24},{20,28},{24,0},{28,4},{1,9},{5... | collective-permute-start | bytes 393224 | tf_op jit(solution)/shard_map/ppermute | solution.py:58
  59.5 12.9 %collective-permute-start.8 = (f32[256,128]{1,0:T(8,128)}, f32[256,128]{1,0:T(8,128)S(1)}, u32[]{:S(2)}, u32[]{:S(2)}) collective-permute-start(f32[256,128]{1,0:T(8,128)} %get-tuple-element.56), channel_id=1, source_target_pairs={{0,12},{4,8},{8,20},{12,16},{16,28},{20,24},{24,4},{28,0},{1,13},{... | collective-permute-start | bytes 393224 | tf_op jit(solution)/shard_map/ppermute | solution.py:58
  68.9 77.8 %collective-permute-start = (f32[1024,256]{0,1:T(8,128)}, f32[1024,256]{0,1:T(8,128)S(1)}, u32[]{:S(2)}, u32[]{:S(2)}) collective-permute-start(f32[1024,256]{0,1:T(8,128)} %pad_maximum_fusion.1), channel_id=1, source_target_pairs={{0,1},{1,0},{2,3},{3,2},{4,5},{5,4},{6,7},{7,6},{8,9},{9,8},{10,11... | collective-permute-start | bytes 3145736 | tf_op jit(solution)/shard_map/ppermute | solution.py:58
  80.5 54.4 %collective-permute-start.10 = (f32[256,128]{1,0:T(8,128)}, f32[256,128]{1,0:T(8,128)S(1)}, u32[]{:S(2)}, u32[]{:S(2)}) collective-permute-start(f32[256,128]{1,0:T(8,128)} %get-tuple-element.56), channel_id=1, source_target_pairs={{0,20},{4,16},{8,28},{12,24},{16,4},{20,0},{24,12},{28,8},{1,21},{... | collective-permute-start | bytes 393224 | tf_op jit(solution)/shard_map/ppermute | solution.py:58
  80.5 67.3 %collective-permute-start.31 = (bf16[256,2048]{1,0:T(8,128)(2,1)}, bf16[256,2048]{1,0:T(8,128)(2,1)S(1)}, u32[]{:S(2)}, u32[]{:S(2)}) collective-permute-start(bf16[256,2048]{1,0:T(8,128)(2,1)} %collective-permute-done.29.refs_6_), channel_id=1, source_target_pairs={{0,8},{4,12},{8,16},{12,20},{16,24},{20,28},{24,0},{28,4},{1,9},{5... | collective-permute-start | bytes 3145736 | tf_op jit(solution)/shard_map/ppermute | solution.py:58
  83.5 65.5 %collective-permute-start.23 = (bf16[256,2048]{1,0:T(8,128)(2,1)}, bf16[256,2048]{1,0:T(8,128)(2,1)S(1)}, u32[]{:S(2)}, u32[]{:S(2)}) collective-permute-start(bf16[256,2048]{1,0:T(8,128)(2,1)} %collective-permute-done.21.refs_6_), channel_id=1, source_target_pairs={{0,8},{4,12},{8,16},{12,20},{16,24},{20,28},{24,0},{28,4},{1,9},{5... | collective-permute-start | bytes 3145736 | tf_op jit(solution)/shard_map/ppermute | solution.py:58
  146.7 12.0 %collective-permute-start.1 = (f32[1024,128]{0,1:T(8,128)S(1)}, f32[1024,128]{0,1:T(8,128)S(1)}, u32[]{:S(2)}, u32[]{:S(2)}) collective-permute-start(f32[1024,128]{0,1:T(8,128)S(1)} %slice_add_fusion), channel_id=1, source_target_pairs={{0,2},{1,3},{2,0},{3,1},{4,6},{5,7},{6,4},{7,5},{8,10},{9,11},{10,... | collective-permute-start | bytes 1572872 | tf_op jit(solution)/shard_map/ppermute | solution.py:58
  147.8 27.9 %collective-permute-start.33 = (bf16[256,2048]{1,0:T(8,128)(2,1)S(1)}, bf16[256,2048]{1,0:T(8,128)(2,1)S(1)}, u32[]{:S(2)}, u32[]{:S(2)}) collective-permute-start(bf16[256,2048]{1,0:T(8,128)(2,1)S(1)} %collective-permute-done.31.refs_8_), channel_id=1, source_target_pairs={{0,8},{4,12},{8,16},{12,20},{16,24},{20,28},{24,0},{28,4},{1,9},{5... | collective-permute-start | bytes 3145736 | tf_op jit(solution)/shard_map/ppermute | solution.py:58
  147.8 29.2 %collective-permute-start.32 = (bf16[256,2048]{1,0:T(8,128)(2,1)S(1)}, bf16[256,2048]{1,0:T(8,128)(2,1)S(1)}, u32[]{:S(2)}, u32[]{:S(2)}) collective-permute-start(bf16[256,2048]{1,0:T(8,128)(2,1)S(1)} %collective-permute-done.31.refs_8_), channel_id=1, source_target_pairs={{0,4},{4,0},{8,12},{12,8},{16,20},{20,16},{24,28},{28,24},{1,5},{5... | collective-permute-start | bytes 3145736 | tf_op jit(solution)/shard_map/ppermute | solution.py:58
  149.1 49.1 %collective-permute-start.25 = (bf16[256,2048]{1,0:T(8,128)(2,1)S(1)}, bf16[256,2048]{1,0:T(8,128)(2,1)S(1)}, u32[]{:S(2)}, u32[]{:S(2)}) collective-permute-start(bf16[256,2048]{1,0:T(8,128)(2,1)S(1)} %collective-permute-done.23.refs_8_), channel_id=1, source_target_pairs={{0,8},{4,12},{8,16},{12,20},{16,24},{20,28},{24,0},{28,4},{1,9},{5... | collective-permute-start | bytes 3145736 | tf_op jit(solution)/shard_map/ppermute | solution.py:58
  149.7 49.8 %collective-permute-start.24 = (bf16[256,2048]{1,0:T(8,128)(2,1)S(1)}, bf16[256,2048]{1,0:T(8,128)(2,1)S(1)}, u32[]{:S(2)}, u32[]{:S(2)}) collective-permute-start(bf16[256,2048]{1,0:T(8,128)(2,1)S(1)} %collective-permute-done.23.refs_8_), channel_id=1, source_target_pairs={{0,4},{4,0},{8,12},{12,8},{16,20},{20,16},{24,28},{28,24},{1,5},{5... | collective-permute-start | bytes 3145736 | tf_op jit(solution)/shard_map/ppermute | solution.py:58
  171.7 50.2 %collective-permute-start.14 = (f32[1024,256]{0,1:T(8,128)S(1)}, f32[1024,256]{0,1:T(8,128)S(1)}, u32[]{:S(2)}, u32[]{:S(2)}) collective-permute-start(f32[1024,256]{0,1:T(8,128)S(1)} %pad_maximum_fusion.2), channel_id=1, source_target_pairs={{0,1},{1,0},{2,3},{3,2},{4,5},{5,4},{6,7},{7,6},{8,9},{9,8},{10,11... | collective-permute-start | bytes 3145736 | tf_op jit(solution)/shard_map/ppermute | solution.py:58
  175.7 31.9 %collective-permute-start.34 = (bf16[256,1024]{1,0:T(8,128)(2,1)S(1)}, bf16[256,1024]{1,0:T(8,128)(2,1)S(1)}, u32[]{:S(2)}, u32[]{:S(2)}) collective-permute-start(bf16[256,1024]{1,0:T(8,128)(2,1)S(1)} %slice.205), channel_id=1, source_target_pairs={{0,4},{4,0},{8,12},{12,8},{16,20},{20,16},{24,28},{28,24},{1,5},{5... | collective-permute-start | bytes 1572872 | tf_op jit(solution)/shard_map/ppermute | solution.py:58
  177.0 32.3 %collective-permute-start.35 = (bf16[256,1024]{1,0:T(8,128)(2,1)S(1)}, bf16[256,1024]{1,0:T(8,128)(2,1)S(1)}, u32[]{:S(2)}, u32[]{:S(2)}) collective-permute-start(bf16[256,1024]{1,0:T(8,128)(2,1)S(1)} %slice.206), channel_id=1, source_target_pairs={{0,8},{4,12},{8,16},{12,20},{16,24},{20,28},{24,0},{28,4},{1,9},{5... | collective-permute-start | bytes 1572872 | tf_op jit(solution)/shard_map/ppermute | solution.py:58
  198.2 20.6 %collective-permute-start.26 = (bf16[256,1024]{1,0:T(8,128)(2,1)S(1)}, bf16[256,1024]{1,0:T(8,128)(2,1)S(1)}, u32[]{:S(2)}, u32[]{:S(2)}) collective-permute-start(bf16[256,1024]{1,0:T(8,128)(2,1)S(1)} %slice.203), channel_id=1, source_target_pairs={{0,4},{4,0},{8,12},{12,8},{16,20},{20,16},{24,28},{28,24},{1,5},{5... | collective-permute-start | bytes 1572872 | tf_op jit(solution)/shard_map/ppermute | solution.py:58
  199.5 20.5 %collective-permute-start.27 = (bf16[256,1024]{1,0:T(8,128)(2,1)S(1)}, bf16[256,1024]{1,0:T(8,128)(2,1)S(1)}, u32[]{:S(2)}, u32[]{:S(2)}) collective-permute-start(bf16[256,1024]{1,0:T(8,128)(2,1)S(1)} %slice.204), channel_id=1, source_target_pairs={{0,8},{4,12},{8,16},{12,20},{16,24},{20,28},{24,0},{28,4},{1,9},{5... | collective-permute-start | bytes 1572872 | tf_op jit(solution)/shard_map/ppermute | solution.py:58
  207.6 33.7 %collective-permute-start.28 = (bf16[256,2048]{1,0:T(8,128)(2,1)}, bf16[256,2048]{1,0:T(8,128)(2,1)S(1)}, u32[]{:S(2)}, u32[]{:S(2)}) collective-permute-start(bf16[256,2048]{1,0:T(8,128)(2,1)} %get-tuple-element.67.refs_4_), channel_id=1, source_target_pairs={{0,4},{4,0},{8,12},{12,8},{16,20},{20,16},{24,28},{28,24},{1,5},{5... | collective-permute-start | bytes 3145736 | tf_op jit(solution)/shard_map/ppermute | solution.py:58
  209.4 105.8 %collective-permute-start.20 = (bf16[256,2048]{1,0:T(8,128)(2,1)}, bf16[256,2048]{1,0:T(8,128)(2,1)}, u32[]{:S(2)}, u32[]{:S(2)}) collective-permute-start(bf16[256,2048]{1,0:T(8,128)(2,1)} %get-tuple-element.68.refs_4_), channel_id=1, source_target_pairs={{0,4},{4,0},{8,12},{12,8},{16,20},{20,16},{24,28},{28,24},{1,5},{5... | collective-permute-start | bytes 3145736 | tf_op jit(solution)/shard_map/ppermute | solution.py:58
  218.8 67.5 %collective-permute-start.30 = (bf16[256,2048]{1,0:T(8,128)(2,1)}, bf16[256,2048]{1,0:T(8,128)(2,1)}, u32[]{:S(2)}, u32[]{:S(2)}) collective-permute-start(bf16[256,2048]{1,0:T(8,128)(2,1)} %collective-permute-done.29.refs_6_), channel_id=1, source_target_pairs={{0,4},{4,0},{8,12},{12,8},{16,20},{20,16},{24,28},{28,24},{1,5},{5... | collective-permute-start | bytes 3145736 | tf_op jit(solution)/shard_map/ppermute | solution.py:58
  220.0 95.1 %collective-permute-start.22 = (bf16[256,2048]{1,0:T(8,128)(2,1)}, bf16[256,2048]{1,0:T(8,128)(2,1)S(1)}, u32[]{:S(2)}, u32[]{:S(2)}) collective-permute-start(bf16[256,2048]{1,0:T(8,128)(2,1)} %collective-permute-done.21.refs_6_), channel_id=1, source_target_pairs={{0,4},{4,0},{8,12},{12,8},{16,20},{20,16},{24,28},{28,24},{1,5},{5... | collective-permute-start | bytes 3145736 | tf_op jit(solution)/shard_map/ppermute | solution.py:58
  310.8 33.9 %collective-permute-start.36 = (f32[512,256]{1,0:T(8,128)}, f32[512,256]{1,0:T(8,128)S(1)}, u32[]{:S(2)}, u32[]{:S(2)}) collective-permute-start(f32[512,256]{1,0:T(8,128)} %get-tuple-element.60), channel_id=1, source_target_pairs={{0,4},{4,0},{8,12},{12,8},{16,20},{20,16},{24,28},{28,24},{1,5},{5... | collective-permute-start | bytes 1572872 | tf_op jit(solution)/shard_map/ppermute | solution.py:58
  314.3 27.6 %collective-permute-start.15 = (f32[128,512]{1,0:T(8,128)S(1)}, f32[128,512]{1,0:T(8,128)S(1)}, u32[]{:S(2)}, u32[]{:S(2)}) collective-permute-start(f32[128,512]{1,0:T(8,128)S(1)} %fusion.46), channel_id=1, source_target_pairs={{0,4},{4,0},{8,12},{12,8},{16,20},{20,16},{24,28},{28,24},{1,5},{5... | collective-permute-start | bytes 786440 | tf_op jit(solution)/shard_map/ppermute | solution.py:104
  340.6 16.8 %collective-permute-start.43 = (f32[512,256]{1,0:T(8,128)}, f32[512,256]{1,0:T(8,128)}, u32[]{:S(2)}, u32[]{:S(2)}) collective-permute-start(f32[512,256]{1,0:T(8,128)} %get-tuple-element.64), channel_id=1, source_target_pairs={{0,4},{4,0},{8,12},{12,8},{16,20},{20,16},{24,28},{28,24},{1,5},{5... | collective-permute-start | bytes 1572872 | tf_op jit(solution)/shard_map/ppermute | solution.py:58
  341.9 15.4 %collective-permute-start.16 = (f32[128,512]{1,0:T(8,128)S(1)}, f32[128,512]{1,0:T(8,128)S(1)}, u32[]{:S(2)}, u32[]{:S(2)}) collective-permute-start(f32[128,512]{1,0:T(8,128)S(1)} %add.229), channel_id=1, source_target_pairs={{0,8},{4,12},{8,0},{12,4},{16,24},{20,28},{24,16},{28,20},{1,9},{5... | collective-permute-start | bytes 786440 | tf_op jit(solution)/shard_map/ppermute | solution.py:104
  342.7 50.6 %collective-permute-start.38 = (f32[512,256]{1,0:T(8,128)}, f32[512,256]{1,0:T(8,128)}, u32[]{:S(2)}, u32[]{:S(2)}) collective-permute-start(f32[512,256]{1,0:T(8,128)} %get-tuple-element.59), channel_id=1, source_target_pairs={{0,4},{4,0},{8,12},{12,8},{16,20},{20,16},{24,28},{28,24},{1,5},{5... | collective-permute-start | bytes 1572872 | tf_op jit(solution)/shard_map/ppermute | solution.py:58
  343.9 54.0 %collective-permute-start.45 = (f32[512,256]{1,0:T(8,128)}, f32[512,256]{1,0:T(8,128)}, u32[]{:S(2)}, u32[]{:S(2)}) collective-permute-start(f32[512,256]{1,0:T(8,128)} %get-tuple-element.63), channel_id=1, source_target_pairs={{0,4},{4,0},{8,12},{12,8},{16,20},{20,16},{24,28},{28,24},{1,5},{5... | collective-permute-start | bytes 1572872 | tf_op jit(solution)/shard_map/ppermute | solution.py:58
  346.6 47.8 %collective-permute-start.37 = (f32[512,256]{1,0:T(8,128)}, f32[512,256]{1,0:T(8,128)}, u32[]{:S(2)}, u32[]{:S(2)}) collective-permute-start(f32[512,256]{1,0:T(8,128)} %dynamic-slice_add_fusion.1), channel_id=1, source_target_pairs={{0,8},{4,12},{8,16},{12,20},{16,24},{20,28},{24,0},{28,4},{1,9},{5... | collective-permute-start | bytes 1572872 | tf_op jit(solution)/shard_map/ppermute | solution.py:58
  357.3 32.6 %collective-permute-start.17 = (f32[128,512]{1,0:T(8,128)S(1)}, f32[128,512]{1,0:T(8,128)S(1)}, u32[]{:S(2)}, u32[]{:S(2)}) collective-permute-start(f32[128,512]{1,0:T(8,128)S(1)} %add.230), channel_id=1, source_target_pairs={{0,16},{4,20},{8,24},{12,28},{16,0},{20,4},{24,8},{28,12},{1,17},{... | collective-permute-start | bytes 786440 | tf_op jit(solution)/shard_map/ppermute | solution.py:104
  359.5 38.3 %collective-permute-start.44 = (f32[512,256]{1,0:T(8,128)}, f32[512,256]{1,0:T(8,128)}, u32[]{:S(2)}, u32[]{:S(2)}) collective-permute-start(f32[512,256]{1,0:T(8,128)} %dynamic-slice_add_fusion), channel_id=1, source_target_pairs={{0,8},{4,12},{8,16},{12,20},{16,24},{20,28},{24,0},{28,4},{1,9},{5... | collective-permute-start | bytes 1572872 | tf_op jit(solution)/shard_map/ppermute | solution.py:58
  390.6 12.3 %collective-permute-start.40 = (f32[512,256]{1,0:T(8,128)}, f32[512,256]{1,0:T(8,128)}, u32[]{:S(2)}, u32[]{:S(2)}) collective-permute-start(f32[512,256]{1,0:T(8,128)} %get-tuple-element.58), channel_id=1, source_target_pairs={{0,4},{4,0},{8,12},{12,8},{16,20},{20,16},{24,28},{28,24},{1,5},{5... | collective-permute-start | bytes 1572872 | tf_op jit(solution)/shard_map/ppermute | solution.py:58
  393.3 17.3 %collective-permute-start.47 = (f32[512,256]{1,0:T(8,128)}, f32[512,256]{1,0:T(8,128)}, u32[]{:S(2)}, u32[]{:S(2)}) collective-permute-start(f32[512,256]{1,0:T(8,128)} %get-tuple-element.62), channel_id=1, source_target_pairs={{0,4},{4,0},{8,12},{12,8},{16,20},{20,16},{24,28},{28,24},{1,5},{5... | collective-permute-start | bytes 1572872 | tf_op jit(solution)/shard_map/ppermute | solution.py:58
  397.8 11.3 %collective-permute-start.39 = (f32[512,256]{1,0:T(8,128)}, f32[512,256]{1,0:T(8,128)}, u32[]{:S(2)}, u32[]{:S(2)}) collective-permute-start(f32[512,256]{1,0:T(8,128)} %add_add_fusion.5), channel_id=1, source_target_pairs={{0,8},{4,12},{8,16},{12,20},{16,24},{20,28},{24,0},{28,4},{1,9},{5... | collective-permute-start | bytes 1572872 | tf_op jit(solution)/shard_map/ppermute | solution.py:58
  400.1 14.6 %collective-permute-start.46 = (f32[512,256]{1,0:T(8,128)}, f32[512,256]{1,0:T(8,128)}, u32[]{:S(2)}, u32[]{:S(2)}) collective-permute-start(f32[512,256]{1,0:T(8,128)} %add_add_fusion.2), channel_id=1, source_target_pairs={{0,8},{4,12},{8,16},{12,20},{16,24},{20,28},{24,0},{28,4},{1,9},{5... | collective-permute-start | bytes 1572872 | tf_op jit(solution)/shard_map/ppermute | solution.py:58
  401.1 59.1 %collective-permute-start.42 = (f32[512,256]{1,0:T(8,128)}, f32[512,256]{1,0:T(8,128)S(1)}, u32[]{:S(2)}, u32[]{:S(2)}) collective-permute-start(f32[512,256]{1,0:T(8,128)} %get-tuple-element.57), channel_id=1, source_target_pairs={{0,4},{4,0},{8,12},{12,8},{16,20},{20,16},{24,28},{28,24},{1,5},{5... | collective-permute-start | bytes 1572872 | tf_op jit(solution)/shard_map/ppermute | solution.py:58
  402.9 58.4 %collective-permute-start.49 = (f32[512,256]{1,0:T(8,128)}, f32[512,256]{1,0:T(8,128)S(1)}, u32[]{:S(2)}, u32[]{:S(2)}) collective-permute-start(f32[512,256]{1,0:T(8,128)} %get-tuple-element.61), channel_id=1, source_target_pairs={{0,4},{4,0},{8,12},{12,8},{16,20},{20,16},{24,28},{28,24},{1,5},{5... | collective-permute-start | bytes 1572872 | tf_op jit(solution)/shard_map/ppermute | solution.py:58
  410.6 49.5 %collective-permute-start.41 = (f32[512,256]{1,0:T(8,128)S(1)}, f32[512,256]{1,0:T(8,128)S(1)}, u32[]{:S(2)}, u32[]{:S(2)}) collective-permute-start(f32[512,256]{1,0:T(8,128)S(1)} %add_add_fusion.4), channel_id=1, source_target_pairs={{0,8},{4,12},{8,16},{12,20},{16,24},{20,28},{24,0},{28,4},{1,9},{5... | collective-permute-start | bytes 1572872 | tf_op jit(solution)/shard_map/ppermute | solution.py:58
  416.2 45.1 %collective-permute-start.48 = (f32[512,256]{1,0:T(8,128)S(1)}, f32[512,256]{1,0:T(8,128)S(1)}, u32[]{:S(2)}, u32[]{:S(2)}) collective-permute-start(f32[512,256]{1,0:T(8,128)S(1)} %add_add_fusion.1), channel_id=1, source_target_pairs={{0,8},{4,12},{8,16},{12,20},{16,24},{20,28},{24,0},{28,4},{1,9},{5... | collective-permute-start | bytes 1572872 | tf_op jit(solution)/shard_map/ppermute | solution.py:58
  470.7 12.2 %collective-permute-start.51 = (f16[528,512]{1,0:T(8,128)(2,1)S(1)}, f16[528,512]{1,0:T(8,128)(2,1)S(1)}, u32[]{:S(2)}, u32[]{:S(2)}) collective-permute-start(f16[528,512]{1,0:T(8,128)(2,1)S(1)} %pad_maximum_fusion.5), channel_id=1, source_target_pairs={{0,8},{4,12},{8,16},{12,20},{16,24},{20,28},{24,0},{28,4},{1,9},{5... | collective-permute-start | bytes 1622024 | tf_op jit(solution)/shard_map/ppermute | solution.py:58
  490.6 11.2 %collective-permute-start.53 = (f16[528,512]{1,0:T(8,128)(2,1)S(1)}, f16[528,512]{1,0:T(8,128)(2,1)S(1)}, u32[]{:S(2)}, u32[]{:S(2)}) collective-permute-start(f16[528,512]{1,0:T(8,128)(2,1)S(1)} %collective-permute-done.51), channel_id=1, source_target_pairs={{0,8},{4,12},{8,16},{12,20},{16,24},{20,28},{24,0},{28,4},{1,9},{5... | collective-permute-start | bytes 1622024 | tf_op jit(solution)/shard_map/ppermute | solution.py:58
  501.8 13.3 %collective-permute-start.55 = (f16[528,512]{1,0:T(8,128)(2,1)S(1)}, f16[528,512]{1,0:T(8,128)(2,1)S(1)}, u32[]{:S(2)}, u32[]{:S(2)}) collective-permute-start(f16[528,512]{1,0:T(8,128)(2,1)S(1)} %collective-permute-done.53), channel_id=1, source_target_pairs={{0,8},{4,12},{8,16},{12,20},{16,24},{20,28},{24,0},{28,4},{1,9},{5... | collective-permute-start | bytes 1622024 | tf_op jit(solution)/shard_map/ppermute | solution.py:58
  503.4 12.7 %collective-permute-start.54 = (f16[528,512]{1,0:T(8,128)(2,1)S(1)}, f16[528,512]{1,0:T(8,128)(2,1)S(1)}, u32[]{:S(2)}, u32[]{:S(2)}) collective-permute-start(f16[528,512]{1,0:T(8,128)(2,1)S(1)} %collective-permute-done.53), channel_id=1, source_target_pairs={{0,4},{4,0},{8,12},{12,8},{16,20},{20,16},{24,28},{28,24},{1,5},{5... | collective-permute-start | bytes 1622024 | tf_op jit(solution)/shard_map/ppermute | solution.py:58
  515.1 12.1 %collective-permute-start.56 = (f16[528,256]{1,0:T(8,128)(2,1)S(1)}, f16[528,256]{1,0:T(8,128)(2,1)S(1)}, u32[]{:S(2)}, u32[]{:S(2)}) collective-permute-start(f16[528,256]{1,0:T(8,128)(2,1)S(1)} %slice.233), channel_id=1, source_target_pairs={{0,4},{4,0},{8,12},{12,8},{16,20},{20,16},{24,28},{28,24},{1,5},{5... | collective-permute-start | bytes 811016 | tf_op jit(solution)/shard_map/ppermute | solution.py:58
  516.1 11.2 %collective-permute-start.57 = (f16[528,256]{1,0:T(8,128)(2,1)S(1)}, f16[528,256]{1,0:T(8,128)(2,1)S(1)}, u32[]{:S(2)}, u32[]{:S(2)}) collective-permute-start(f16[528,256]{1,0:T(8,128)(2,1)S(1)} %slice.234), channel_id=1, source_target_pairs={{0,8},{4,12},{8,16},{12,20},{16,24},{20,28},{24,0},{28,4},{1,9},{5... | collective-permute-start | bytes 811016 | tf_op jit(solution)/shard_map/ppermute | solution.py:58
  (27 other events, 388.8 us)

commit v2 on v1

--- a/solution.py
+++ b/solution.py
@@ -188,84 +188,55 @@
     )(*args)
 
 
-def feedback_kernel(places, ortho, buffer, *refs):
+def output_kernel(places, ortho, q_hi, q_lo, inv_norm, buffer, right, *refs):
     del places
-    rights, (out, squares) = refs[:-2], refs[-2:]
-    for k, right in enumerate(rights):
-
-        @pl.when(pl.program_id(0) == k)
-        def _(right=right):
-            product = dot(ortho[...], right[...].astype(BF16), 1, 1)
-            out[...] = buffer[...] - product
-            square = jnp.sum(right[...] * right[...], axis=0, keepdims=True)
-            squares[...] = square if k == 0 else squares[...] + square
-
-
-def feedback_call(ortho, buffer, rights, places):
-    rows = buffer.shape[0]
-    strip, rank = rights[0].shape
+    momentum, normalized, update = refs[-3:]
+    value = right[...]
+    hi = value.astype(BF16)
+    lo = (value - hi.astype(F32)).astype(BF16)
+    momentum[...] = buffer[...] - dot(ortho[...], hi, 1, 1)
+    normalized[...] = value * inv_norm[...]
+    product = dot(q_hi[...], hi, 1, 1) + dot(q_hi[...], lo, 1, 1) + dot(q_lo[...], hi, 1, 1)
+    update[...] = product.astype(BF16)
+
+
+def output_call(ortho, q_hi, q_lo, inv_norm, outs, right, places, strip):
+    rows, columns = outs[0].shape
+    rank = right.shape[1]
+    count = right.shape[0] // strip
     whole = lambda a: pl.BlockSpec(a.shape, lambda k, p: (0, 0), pipeline_mode=pl.Buffered(1))
     placed = pl.BlockSpec((rows, strip), lambda k, p: (0, p[k]))
-    count = len(rights)
+    fixed = [ortho, q_hi, q_lo, inv_norm]
+    args = [places, *fixed, outs[0], right, *outs[1:]]
+    in_specs = [whole(a) for a in fixed] + [placed]
+    in_specs += [pl.BlockSpec((strip, rank), lambda k, p: (k, 0))]
+    in_specs += [pl.BlockSpec(memory_space=pl.ANY) for _ in outs[1:]]
+    aliases = {5: 0}
+    aliases.update({7 + k: 1 + k for k in range(len(outs) - 1)})
     return pl.pallas_call(
-        feedback_kernel,
+        output_kernel,
         grid_spec=pltpu.PrefetchScalarGridSpec(
             num_scalar_prefetch=1,
             grid=(count,),
-            in_specs=[whole(ortho), placed] + [whole(r) for r in rights],
-            out_specs=[placed, pl.BlockSpec((1, rank), lambda k, p: (0, 0))],
+            in_specs=in_specs,
+            out_specs=[placed, pl.BlockSpec((strip, rank), lambda k, p: (p[k], 0)), placed],
         ),
         out_shape=[
-            jax.ShapeDtypeStruct(buffer.shape, F32),
-            jax.ShapeDtypeStruct((1, rank), F32),
+            jax.ShapeDtypeStruct((rows, columns), F32),
+            jax.ShapeDtypeStruct((columns, rank), F32),
+            jax.ShapeDtypeStruct((rows, columns), BF16),
         ],
-        input_output_aliases={2: 0},
+        input_output_aliases=aliases,
         compiler_params=pltpu.CompilerParams(
             dimension_semantics=("arbitrary",), vmem_limit_bytes=32 << 20
         ),
         cost_estimate=pl.CostEstimate(
-            flops=2 * rows * strip * rank * count,
+            flops=8 * rows * strip * rank * count,
             transcendentals=0,
-            bytes_accessed=8 * rows * strip * count,
+            bytes_accessed=10 * rows * strip * count,
         ),
-        name="feedback",
-    )(places, ortho, buffer, *rights)
-
-
-def update_kernel(q_hi, q_lo, inv_norm, raw, update, right):
-    value = raw[...]
-    right[...] = value * inv_norm[...]
-    hi = value.astype(BF16)
-    lo = (value - hi.astype(F32)).astype(BF16)
-    product = dot(q_hi[...], hi, 1, 1) + dot(q_hi[...], lo, 1, 1) + dot(q_lo[...], hi, 1, 1)
-    update[...] = product.astype(BF16)
-
-
-def update_call(q_hi, q_lo, inv_norm, raw):
-    rows, rank = q_hi.shape
-    columns = raw.shape[0]
-    tile = min(TILE, columns)
-    whole = lambda a: pl.BlockSpec(a.shape, lambda j: (0, 0), pipeline_mode=pl.Buffered(1))
-    tall = pl.BlockSpec((tile, rank), lambda j: (j, 0))
-    return pl.pallas_call(
-        update_kernel,
-        grid=(columns // tile,),
-        in_specs=[whole(q_hi), whole(q_lo), whole(inv_norm), tall],
-        out_specs=[pl.BlockSpec((rows, tile), lambda j: (0, j)), tall],
-        out_shape=[
-            jax.ShapeDtypeStruct((rows, columns), BF16),
-            jax.ShapeDtypeStruct((columns, rank), F32),
-        ],
-        compiler_params=pltpu.CompilerParams(
-            dimension_semantics=("arbitrary",), vmem_limit_bytes=40 << 20
-        ),
-        cost_estimate=pl.CostEstimate(
-            flops=6 * rows * columns * rank,
-            transcendentals=0,
-            bytes_accessed=columns * (2 * rows + 8 * rank),
-        ),
-        name="update",
-    )(q_hi, q_lo, inv_norm, raw)
+        name="outputs",
+    )(*args)
 
 
 def eliminate(block, unroll):
@@ -393,29 +364,23 @@
         ],
         axis=0,
     )
+    col_squares = wide.total(narrow.total(own[None, :]))
     feedback_left = (FEEDBACK * ortho).astype(BF16)
     gathered = dict(zip(wide.order(), wide.gather(sent, spread=wide.inner == 2)))
-    pieces, starts, squares = [], [], []
+    inv_norm = 1.0 / (jnp.sqrt(col_squares) + EPSILON)
+    q_hi, q_lo = split(ortho * (math.sqrt(dout * din / rank) * inv_norm))
+    outs = [buffer]
     for s in range(wide.outer):
         rights, places = [], []
         for d in range(wide.inner):
             got = gathered[s, d]
-            value = got[:-PAD].astype(F32) * jnp.exp2(got[-PAD : -PAD + 1].astype(F32))
-            value = lax.optimization_barrier(value)
-            for h in range(halves):
-                place = h * members + wide.at(-s, -d)
-                rights.append(value[h * strip : (h + 1) * strip])
-                places.append(place)
-                starts.append(place * strip)
-        pieces += rights
-        buffer, square = feedback_call(feedback_left, buffer, rights, jnp.stack(places))
-        squares.append(square)
-    raw = put(pieces, starts, (columns, rank), 0)
-    col_squares = narrow.total(sum(squares))
-    inv_norm = 1.0 / (jnp.sqrt(col_squares) + EPSILON)
-    q_hi, q_lo = split(ortho * (math.sqrt(dout * din / rank) * inv_norm))
-    update, new_right = update_call(q_hi, q_lo, inv_norm, raw)
-    return buffer, new_right, update
+            rights.append(got[:-PAD].astype(F32) * jnp.exp2(got[-PAD : -PAD + 1].astype(F32)))
+            places += [h * members + wide.at(-s, -d) for h in range(halves)]
+        right = lax.optimization_barrier(jnp.concatenate(rights, axis=0))
+        outs = output_call(
+            feedback_left, q_hi, q_lo, inv_norm, outs, right, jnp.stack(places), strip
+        )
+    return tuple(outs)
 
 
 def solution(mesh):

time: 565 us -> 579 us (1.025)
  waiting for transfers between devices: 277 us -> 304 us
  Pallas kernels: 128 us -> 118 us
    ppermute x5 -> x8, waiting for transfers between devices: 43.1 us -> 61.2 us  [total(): got = lax.ppermute(x, self.name, [(k, k ^ step) for k in range(count)])]
    pallas_call x5 -> x4, Pallas kernels: 41.4 us -> 32.1 us  [output_call(): pl.pallas_call(output_kernel, grid_spec=pltpu.PrefetchScalarGridSpec(num_...]
    ppermute x55, waiting for transfers between devices: 234 us -> 243 us  [send(): return lax.ppermute(x, self.name, pairs)]
  transfers between devices with their start and end apart: 60 -> 63, of which waited for: 29 -> 34; matrix products, arithmetic and copies ran while one was open for 15% -> 13% of each run, Pallas kernels for 19% -> 16%
where the time goes in v2:
time: 579 us; the launch traced here: 569 us
  waiting for transfers between devices  304 us (53%)
  Pallas kernels  118 us (20%)
  starting transfers between devices  56.9 us (10%)
  matrix products  40 us (7%)
  other arithmetic  29.6 us (5%)
  local copies, waits for them, and re-layouts  18 us (3%)
    ppermute x55, waiting for transfers between devices, send(): return lax.ppermute(x, self.name, pairs)  243 us
    ppermute x8, waiting for transfers between devices, total(): got = lax.ppermute(x, self.name, [(k, k ^ step) for k in range(count)])  61.2 us
    ppermute x55, starting transfers between devices, send(): return lax.ppermute(x, self.name, pairs)  51.6 us
    pallas_call x4, Pallas kernels, cholesky_inverse(): pl.pallas_call(lambda *refs, first=first: inverse_kernel(first, size, *re...  43.2 us
    pallas_call x2, Pallas kernels, buffer_call(): pl.pallas_call(lambda *refs: buffer_kernel(count, *refs), grid=(width //...  43.1 us
    dot_general x8, matrix products, dot(): lax.dot_general(a, b, (((ca,), (cb,)), ((), ())), precision=precision, pr...  40 us
    pallas_call x4, Pallas kernels, output_call(): pl.pallas_call(output_kernel, grid_spec=pltpu.PrefetchScalarGridSpec(num_...  32.1 us
  transfers between devices with their start and end apart: 63, of which 34 were waited for; matrix products, arithmetic and copies ran while one was open for 13% of the time, Pallas kernels for 16%

profile of v2, /device:TPU:0, one launch (start us, length us, event | category | flops | bytes accessed | tf_op | source)
XLA Modules:
  0.0 569.1 jit_solution(1905013489568729423)
XLA Ops:
  2.2 3.1 collective-permute-start.2
  5.2 5.3 fusion.3
  21.0 8.4 %collective-permute-done.2 = bf16[512,1024]{0,1:T(8,128)(2,1)} collective-permute-done((bf16[512,1024]{0,1:T(8,128)(2,1)S(1)}, bf16[512,1024]{0,1:T(8,128)(2,1)}, u32[]{:S(2)}, u32[]{:S(2)}) %collective-permute-start.2) | collective-permute-done | bytes 1048608 | tf_op jit(solution)/shard_map/ppermute | solution.py:58
  29.3 2.8 pad_maximum_fusion
  32.1 19.3 %fusion.45 = f32[1024,512]{0,1:T(8,128)} fusion(f32[1024,4096]{1,0:T(8,128)} %refs_3_.3, f32[4096,512]{1,0:T(8,128)} %param.7), kind=kOutput, calls=%fused_computation.138 | convolution fusion | flops 12884901888 | bytes 27262976 | tf_op jit(solution)/shard_map/dot_general | solution.py:33
  59.5 2.8 collective-permute-start.8
  63.3 5.6 collective-permute-done.7
  68.9 3.5 collective-permute-done.8
  73.8 6.7 %collective-permute-done.9 = f32[256,128]{1,0:T(8,128)S(1)} collective-permute-done((f32[256,128]{1,0:T(8,128)}, f32[256,128]{1,0:T(8,128)S(1)}, u32[]{:S(2)}, u32[]{:S(2)}) %collective-permute-start.9) | collective-permute-done | bytes 131104 | tf_op jit(solution)/shard_map/ppermute | solution.py:58
  80.5 3.0 collective-permute-start.38
  84.2 50.7 %collective-permute-done.10 = f32[256,128]{1,0:T(8,128)S(1)} collective-permute-done((f32[256,128]{1,0:T(8,128)}, f32[256,128]{1,0:T(8,128)S(1)}, u32[]{:S(2)}, u32[]{:S(2)}) %collective-permute-start.10) | collective-permute-done | bytes 131104 | tf_op jit(solution)/shard_map/ppermute | solution.py:58
  134.9 5.6 collective-permute-done.11
  140.5 2.7 collective-permute-start.12
  143.3 3.3 collective-permute-done.12
  161.6 10.1 %collective-permute-done.13 = f32[1024,128]{0,1:T(8,128)S(1)} collective-permute-done((f32[1024,128]{0,1:T(8,128)S(1)}, f32[1024,128]{0,1:T(8,128)S(1)}, u32[]{:S(2)}, u32[]{:S(2)}) %collective-permute-start.13) | collective-permute-done | bytes 524320 | tf_op jit(solution)/shard_map/ppermute | solution.py:58
  174.4 2.5 collective-permute-done.40.refs_10_
  177.8 18.5 %collective-permute-done.24.refs_9_ = bf16[256,2048]{1,0:T(8,128)(2,1)S(1)} collective-permute-done((bf16[256,2048]{1,0:T(8,128)(2,1)S(1)}, bf16[256,2048]{1,0:T(8,128)(2,1)S(1)}, u32[]{:S(2)}, u32[]{:S(2)}) %collective-permute-start.24) | collective-permute-done | bytes 1048608 | tf_op jit(solution)/shard_map/ppermute | solution.py:58
  196.4 2.9 collective-permute-done.25.refs_10_
  200.3 10.3 %collective-permute-done.42 = bf16[256,1024]{1,0:T(8,128)(2,1)S(1)} collective-permute-done((bf16[256,1024]{1,0:T(8,128)(2,1)S(1)}, bf16[256,1024]{1,0:T(8,128)(2,1)S(1)}, u32[]{:S(2)}, u32[]{:S(2)}) %collective-permute-start.42) | collective-permute-done | bytes 524320 | tf_op jit(solution)/shard_map/ppermute | solution.py:58
  213.7 5.2 collective-permute-done.27
  223.9 39.9 %collective-permute-done.20.refs_5_ = bf16[256,2048]{1,0:T(8,128)(2,1)} collective-permute-done((bf16[256,2048]{1,0:T(8,128)(2,1)}, bf16[256,2048]{1,0:T(8,128)(2,1)}, u32[]{:S(2)}, u32[]{:S(2)}) %collective-permute-start.20) | collective-permute-done | bytes 1048608 | tf_op jit(solution)/shard_map/ppermute | solution.py:58
  263.8 41.7 %collective-permute-done.22.refs_7_ = bf16[256,2048]{1,0:T(8,128)(2,1)S(1)} collective-permute-done((bf16[256,2048]{1,0:T(8,128)(2,1)}, bf16[256,2048]{1,0:T(8,128)(2,1)S(1)}, u32[]{:S(2)}, u32[]{:S(2)}) %collective-permute-start.22) | collective-permute-done | bytes 1048608 | tf_op jit(solution)/shard_map/ppermute | solution.py:58
  306.4 21.6 %buffer_product.2 = (f32[1024,4096]{1,0:T(8,128)}, f32[512,2048]{1,0:T(8,128)}) custom-call(bf16[1024,2048]{1,0:T(8,128)(2,1)} %bitcast.44, bf16[512,1024]{1,0:T(8,128)(2,1)} %get-tuple-element.69.refs_1_, bf16[512,1024]{1,0:T(8,128)(2,1)} %get-tuple-element.68.refs_2_, f32[1024,4096]{1,0:T(8,128)} %refs_3_.3, bf16[256,2048]{1,0:T(8,128)(2,1)} %get-tuple-element.66.refs_4_, ...), custom_call_target="tpu_custom_call" | custom-call | flops 15032385536 | bytes 29360128 | tf_op jit(solution)/shard_map/buffer_product/pallas_call | solution.py:171
  329.0 21.6 %buffer_product.3 = (f32[1024,4096]{1,0:T(8,128)}, f32[512,2048]{1,0:T(8,128)}) custom-call(bf16[1024,2048]{1,0:T(8,128)(2,1)} %bitcast.45, bf16[512,1024]{1,0:T(8,128)(2,1)} %get-tuple-element.69.refs_1_, bf16[512,1024]{1,0:T(8,128)(2,1)} %get-tuple-element.68.refs_2_, f32[1024,4096]{1,0:T(8,128)} %refs_3_.3, ...), custom_call_target="tpu_custom_call", output_to_operand_aliasing={{0}: (12, {})} | custom-call | flops 15032385536 | bytes 29360128 | tf_op jit(solution)/shard_map/buffer_product/pallas_call | solution.py:171
  350.6 2.9 constant_dynamic-slice_fusion
  360.2 13.7 %collective-permute-done.15 = f32[128,512]{1,0:T(8,128)S(1)} collective-permute-done((f32[128,512]{1,0:T(8,128)S(1)}, f32[128,512]{1,0:T(8,128)S(1)}, u32[]{:S(2)}, u32[]{:S(2)}) %collective-permute-start.15) | collective-permute-done | bytes 262176 | tf_op jit(solution)/shard_map/ppermute | solution.py:104
  379.1 7.3 %collective-permute-done.16 = f32[128,512]{1,0:T(8,128)S(1)} collective-permute-done((f32[128,512]{1,0:T(8,128)S(1)}, f32[128,512]{1,0:T(8,128)S(1)}, u32[]{:S(2)}, u32[]{:S(2)}) %collective-permute-start.16) | collective-permute-done | bytes 262176 | tf_op jit(solution)/shard_map/ppermute | solution.py:104
  388.0 31.7 %collective-permute-done.17 = f32[128,512]{1,0:T(8,128)} collective-permute-done((f32[128,512]{1,0:T(8,128)S(1)}, f32[128,512]{1,0:T(8,128)}, u32[]{:S(2)}, u32[]{:S(2)}) %collective-permute-start.17) | collective-permute-done | bytes 262176 | tf_op jit(solution)/shard_map/ppermute | solution.py:104
  424.6 2.3 add_add_fusion.2
  426.9 2.3 add_add_fusion.5
  433.2 5.0 collective-permute-done.46
  439.7 4.1 collective-permute-done.31
  445.6 11.6 %cholesky_inverse.4 = (f32[512,512]{1,0:T(8,128)S(1)}, f32[512,512]{1,0:T(8,128)S(1)}) custom-call(f32[512,512]{1,0:T(8,128)S(1)} %slice_dynamic-update-slice_fusion.4.refs_0_), custom_call_target="tpu_custom_call" | custom-call | tf_op jit(solution)/shard_map/cholesky_inverse/pallas_call | solution.py:298
  457.2 11.0 %cholesky_inverse.5 = (f32[512,512]{1,0:T(8,128)S(1)}, f32[512,512]{1,0:T(8,128)S(1)}) custom-call(f32[512,512]{1,0:T(8,128)S(1)} %get-tuple-element.23.refs_0_, f32[512,512]{1,0:T(8,128)S(1)} %get-tuple-element.24.refs_1_), custom_call_target="tpu_custom_call" | custom-call | tf_op jit(solution)/shard_map/cholesky_inverse/pallas_call | solution.py:298
  468.2 10.6 %cholesky_inverse.6 = (f32[512,512]{1,0:T(8,128)S(1)}, f32[512,512]{1,0:T(8,128)S(1)}) custom-call(f32[512,512]{1,0:T(8,128)S(1)} %get-tuple-element.25.refs_0_, f32[512,512]{1,0:T(8,128)S(1)} %get-tuple-element.26.refs_1_), custom_call_target="tpu_custom_call" | custom-call | tf_op jit(solution)/shard_map/cholesky_inverse/pallas_call | solution.py:298
  478.9 10.0 %cholesky_inverse.7 = (f32[512,512]{1,0:T(8,128)}, f32[512,512]{1,0:T(8,128)S(1)}) custom-call(f32[512,512]{1,0:T(8,128)S(1)} %get-tuple-element.27.refs_0_, f32[512,512]{1,0:T(8,128)S(1)} %get-tuple-element.28.refs_1_), custom_call_target="tpu_custom_call" | custom-call | tf_op jit(solution)/shard_map/cholesky_inverse/pallas_call | solution.py:298
  491.2 4.5 multiply_reduce_fusion
  497.9 2.5 collective-permute-done.51
  501.3 2.7 collective-permute-done.52
  507.7 2.3 collective-permute-start.54
  513.3 3.6 fusion.5
  516.9 4.7 collective-permute-done.55
  521.9 2.3 collective-permute-done.56
  525.6 8.0 %outputs.4 = (f32[1024,4096]{1,0:T(8,128)}, f32[4096,512]{1,0:T(8,128)}, bf16[1024,4096]{1,0:T(8,128)(2,1)}) custom-call(s32[4]{0:T(128)S(1)} %pad_add_fusion.3.places, bf16[1024,512]{1,0:T(8,128)(2,1)S(1)} %get-tuple-element.65.ortho, bf16[1024,512]{1,0:T(8,128)(2,1)S(1)} %get-tuple-element.64.q_hi, ...), custom_call_target="tpu_custom_call", output_to_operand_aliasing={{0}: (5, {})} | custom-call | flops 4294967296 | bytes 10485760 | tf_op jit(solution)/shard_map/outputs/pallas_call | solution.py:216
  534.8 2.4 collective-permute-done.58
  538.3 8.0 %outputs.5 = (f32[1024,4096]{1,0:T(8,128)}, f32[4096,512]{1,0:T(8,128)}, bf16[1024,4096]{1,0:T(8,128)(2,1)}) custom-call(s32[4]{0:T(128)S(1)} %pad_add_fusion.2.places, bf16[1024,512]{1,0:T(8,128)(2,1)S(1)} %get-tuple-element.65.ortho, bf16[1024,512]{1,0:T(8,128)(2,1)S(1)} %get-tuple-element.64.q_hi, ...), custom_call_target="tpu_custom_call", output_to_operand_aliasing={{0}: (5, {}), {1}: (7, {}), {2}: (8, {})} | custom-call | flops 4294967296 | bytes 10485760 | tf_op jit(solution)/shard_map/outputs/pallas_call | solution.py:216
  552.0 8.0 %outputs.6 = (f32[1024,4096]{1,0:T(8,128)}, f32[4096,512]{1,0:T(8,128)}, bf16[1024,4096]{1,0:T(8,128)(2,1)}) custom-call(s32[4]{0:T(128)S(1)} %pad_add_fusion.1.places, bf16[1024,512]{1,0:T(8,128)(2,1)S(1)} %get-tuple-element.65.ortho, bf16[1024,512]{1,0:T(8,128)(2,1)S(1)} %get-tuple-element.64.q_hi, ...), custom_call_target="tpu_custom_call", output_to_operand_aliasing={{0}: (5, {}), {1}: (7, {}), {2}: (8, {})} | custom-call | flops 4294967296 | bytes 10485760 | tf_op jit(solution)/shard_map/outputs/pallas_call | solution.py:216
  560.7 8.0 %outputs.7 = (f32[1024,4096]{1,0:T(8,128)}, f32[4096,512]{1,0:T(8,128)}, bf16[1024,4096]{1,0:T(8,128)(2,1)}) custom-call(s32[4]{0:T(128)S(1)} %pad_add_fusion.places, bf16[1024,512]{1,0:T(8,128)(2,1)S(1)} %get-tuple-element.65.ortho, bf16[1024,512]{1,0:T(8,128)(2,1)S(1)} %get-tuple-element.64.q_hi, ...), custom_call_target="tpu_custom_call", output_to_operand_aliasing={{0}: (5, {}), {1}: (7, {}), {2}: (8, {})} | custom-call | flops 4294967296 | bytes 10485760 | tf_op jit(solution)/shard_map/outputs/pallas_call | solution.py:216
  (221 shorter events, 100.8 us)
Async XLA Ops:
  2.2 27.2 %collective-permute-start.2 = (bf16[512,1024]{0,1:T(8,128)(2,1)S(1)}, bf16[512,1024]{0,1:T(8,128)(2,1)}, u32[]{:S(2)}, u32[]{:S(2)}) collective-permute-start(bf16[512,1024]{0,1:T(8,128)(2,1)S(1)} %copy.18), channel_id=1, source_target_pairs={{0,2},{1,3},{2,0},{3,1},{4,6},{5,7},{6,4},{7,5},{8,10},{9,11},{10,... | collective-permute-start | bytes 3145736 | tf_op jit(solution)/shard_map/ppermute | solution.py:58
  15.4 65.1 %collective-permute-start.36 = (bf16[256,2048]{1,0:T(8,128)(2,1)}, bf16[256,2048]{1,0:T(8,128)(2,1)}, u32[]{:S(2)}, u32[]{:S(2)}) collective-permute-start(bf16[256,2048]{1,0:T(8,128)(2,1)} %get-tuple-element.67.refs_4_), channel_id=1, source_target_pairs={{0,8},{4,12},{8,16},{12,20},{16,24},{20,28},{24,0},{28,4},{1,9},{5... | collective-permute-start | bytes 3145736 | tf_op jit(solution)/shard_map/ppermute | solution.py:58
  17.4 66.2 %collective-permute-start.21 = (bf16[256,2048]{1,0:T(8,128)(2,1)}, bf16[256,2048]{1,0:T(8,128)(2,1)}, u32[]{:S(2)}, u32[]{:S(2)}) collective-permute-start(bf16[256,2048]{1,0:T(8,128)(2,1)} %get-tuple-element.66.refs_4_), channel_id=1, source_target_pairs={{0,8},{4,12},{8,16},{12,20},{16,24},{20,28},{24,0},{28,4},{1,9},{5... | collective-permute-start | bytes 3145736 | tf_op jit(solution)/shard_map/ppermute | solution.py:58
  19.9 31.5 %collective-permute-start.5 = (f32[256,128]{1,0:T(8,128)S(1)}, f32[256,128]{1,0:T(8,128)S(1)}, u32[]{:S(2)}, u32[]{:S(2)}) collective-permute-start(f32[256,128]{1,0:T(8,128)S(1)} %slice_add_fusion.2), channel_id=1, source_target_pairs={{0,2},{1,3},{2,0},{3,1},{4,6},{5,7},{6,4},{7,5},{8,10},{9,11},{10,... | collective-permute-start | bytes 393224 | tf_op jit(solution)/shard_map/ppermute | solution.py:58
  32.1 117.8 %collective-permute-start.3 = (bf16[1024,1024]{0,1:T(8,128)(2,1)}, bf16[1024,1024]{0,1:T(8,128)(2,1)}, u32[]{:S(2)}, u32[]{:S(2)}) collective-permute-start(bf16[1024,1024]{0,1:T(8,128)(2,1)} %pad_maximum_fusion), channel_id=1, source_target_pairs={{0,1},{1,0},{2,3},{3,2},{4,5},{5,4},{6,7},{7,6},{8,9},{9,8},{10,11... | collective-permute-start | bytes 6291464 | tf_op jit(solution)/shard_map/ppermute | solution.py:58
  56.4 12.5 %collective-permute-start.7 = (f32[256,128]{1,0:T(8,128)}, f32[256,128]{1,0:T(8,128)S(1)}, u32[]{:S(2)}, u32[]{:S(2)}) collective-permute-start(f32[256,128]{1,0:T(8,128)} %get-tuple-element.54), channel_id=1, source_target_pairs={{0,8},{4,12},{8,16},{12,20},{16,24},{20,28},{24,0},{28,4},{1,9},{5... | collective-permute-start | bytes 393224 | tf_op jit(solution)/shard_map/ppermute | solution.py:58
  59.5 12.9 %collective-permute-start.8 = (f32[256,128]{1,0:T(8,128)}, f32[256,128]{1,0:T(8,128)S(1)}, u32[]{:S(2)}, u32[]{:S(2)}) collective-permute-start(f32[256,128]{1,0:T(8,128)} %get-tuple-element.54), channel_id=1, source_target_pairs={{0,12},{4,8},{8,20},{12,16},{16,28},{20,24},{24,4},{28,0},{1,13},{... | collective-permute-start | bytes 393224 | tf_op jit(solution)/shard_map/ppermute | solution.py:58
  68.9 77.8 %collective-permute-start = (f32[1024,256]{0,1:T(8,128)}, f32[1024,256]{0,1:T(8,128)S(1)}, u32[]{:S(2)}, u32[]{:S(2)}) collective-permute-start(f32[1024,256]{0,1:T(8,128)} %pad_maximum_fusion.5), channel_id=1, source_target_pairs={{0,1},{1,0},{2,3},{3,2},{4,5},{5,4},{6,7},{7,6},{8,9},{9,8},{10,11... | collective-permute-start | bytes 3145736 | tf_op jit(solution)/shard_map/ppermute | solution.py:58
  80.5 54.4 %collective-permute-start.10 = (f32[256,128]{1,0:T(8,128)}, f32[256,128]{1,0:T(8,128)S(1)}, u32[]{:S(2)}, u32[]{:S(2)}) collective-permute-start(f32[256,128]{1,0:T(8,128)} %get-tuple-element.54), channel_id=1, source_target_pairs={{0,20},{4,16},{8,28},{12,24},{16,4},{20,0},{24,12},{28,8},{1,21},{... | collective-permute-start | bytes 393224 | tf_op jit(solution)/shard_map/ppermute | solution.py:58
  80.5 67.3 %collective-permute-start.38 = (bf16[256,2048]{1,0:T(8,128)(2,1)}, bf16[256,2048]{1,0:T(8,128)(2,1)S(1)}, u32[]{:S(2)}, u32[]{:S(2)}) collective-permute-start(bf16[256,2048]{1,0:T(8,128)(2,1)} %collective-permute-done.36.refs_6_), channel_id=1, source_target_pairs={{0,8},{4,12},{8,16},{12,20},{16,24},{20,28},{24,0},{28,4},{1,9},{5... | collective-permute-start | bytes 3145736 | tf_op jit(solution)/shard_map/ppermute | solution.py:58
  83.5 65.4 %collective-permute-start.23 = (bf16[256,2048]{1,0:T(8,128)(2,1)}, bf16[256,2048]{1,0:T(8,128)(2,1)S(1)}, u32[]{:S(2)}, u32[]{:S(2)}) collective-permute-start(bf16[256,2048]{1,0:T(8,128)(2,1)} %collective-permute-done.21.refs_6_), channel_id=1, source_target_pairs={{0,8},{4,12},{8,16},{12,20},{16,24},{20,28},{24,0},{28,4},{1,9},{5... | collective-permute-start | bytes 3145736 | tf_op jit(solution)/shard_map/ppermute | solution.py:58
  146.7 12.0 %collective-permute-start.1 = (f32[1024,128]{0,1:T(8,128)S(1)}, f32[1024,128]{0,1:T(8,128)S(1)}, u32[]{:S(2)}, u32[]{:S(2)}) collective-permute-start(f32[1024,128]{0,1:T(8,128)S(1)} %slice_add_fusion), channel_id=1, source_target_pairs={{0,2},{1,3},{2,0},{3,1},{4,6},{5,7},{6,4},{7,5},{8,10},{9,11},{10,... | collective-permute-start | bytes 1572872 | tf_op jit(solution)/shard_map/ppermute | solution.py:58
  147.8 26.0 %collective-permute-start.39 = (bf16[256,2048]{1,0:T(8,128)(2,1)S(1)}, bf16[256,2048]{1,0:T(8,128)(2,1)S(1)}, u32[]{:S(2)}, u32[]{:S(2)}) collective-permute-start(bf16[256,2048]{1,0:T(8,128)(2,1)S(1)} %collective-permute-done.38.refs_8_), channel_id=1, source_target_pairs={{0,4},{4,0},{8,12},{12,8},{16,20},{20,16},{24,28},{28,24},{1,5},{5... | collective-permute-start | bytes 3145736 | tf_op jit(solution)/shard_map/ppermute | solution.py:58
  149.0 27.9 %collective-permute-start.40 = (bf16[256,2048]{1,0:T(8,128)(2,1)S(1)}, bf16[256,2048]{1,0:T(8,128)(2,1)S(1)}, u32[]{:S(2)}, u32[]{:S(2)}) collective-permute-start(bf16[256,2048]{1,0:T(8,128)(2,1)S(1)} %collective-permute-done.38.refs_8_), channel_id=1, source_target_pairs={{0,8},{4,12},{8,16},{12,20},{16,24},{20,28},{24,0},{28,4},{1,9},{5... | collective-permute-start | bytes 3145736 | tf_op jit(solution)/shard_map/ppermute | solution.py:58
  149.0 47.3 %collective-permute-start.24 = (bf16[256,2048]{1,0:T(8,128)(2,1)S(1)}, bf16[256,2048]{1,0:T(8,128)(2,1)S(1)}, u32[]{:S(2)}, u32[]{:S(2)}) collective-permute-start(bf16[256,2048]{1,0:T(8,128)(2,1)S(1)} %collective-permute-done.23.refs_8_), channel_id=1, source_target_pairs={{0,4},{4,0},{8,12},{12,8},{16,20},{20,16},{24,28},{28,24},{1,5},{5... | collective-permute-start | bytes 3145736 | tf_op jit(solution)/shard_map/ppermute | solution.py:58
  149.9 49.4 %collective-permute-start.25 = (bf16[256,2048]{1,0:T(8,128)(2,1)S(1)}, bf16[256,2048]{1,0:T(8,128)(2,1)S(1)}, u32[]{:S(2)}, u32[]{:S(2)}) collective-permute-start(bf16[256,2048]{1,0:T(8,128)(2,1)S(1)} %collective-permute-done.23.refs_8_), channel_id=1, source_target_pairs={{0,8},{4,12},{8,16},{12,20},{16,24},{20,28},{24,0},{28,4},{1,9},{5... | collective-permute-start | bytes 3145736 | tf_op jit(solution)/shard_map/ppermute | solution.py:58
  160.5 11.1 %collective-permute-start.13 = (f32[1024,128]{0,1:T(8,128)S(1)}, f32[1024,128]{0,1:T(8,128)S(1)}, u32[]{:S(2)}, u32[]{:S(2)}) collective-permute-start(f32[1024,128]{0,1:T(8,128)S(1)} %get-tuple-element.52), channel_id=1, source_target_pairs={{0,2},{1,3},{2,0},{3,1},{4,6},{5,7},{6,4},{7,5},{8,10},{9,11},{10,... | collective-permute-start | bytes 1572872 | tf_op jit(solution)/shard_map/ppermute | solution.py:58
  171.7 50.2 %collective-permute-start.14 = (f32[1024,256]{0,1:T(8,128)S(1)}, f32[1024,256]{0,1:T(8,128)S(1)}, u32[]{:S(2)}, u32[]{:S(2)}) collective-permute-start(f32[1024,256]{0,1:T(8,128)S(1)} %pad_maximum_fusion.6), channel_id=1, source_target_pairs={{0,1},{1,0},{2,3},{3,2},{4,5},{5,4},{6,7},{7,6},{8,9},{9,8},{10,11... | collective-permute-start | bytes 3145736 | tf_op jit(solution)/shard_map/ppermute | solution.py:58
  173.9 36.7 %collective-permute-start.42 = (bf16[256,1024]{1,0:T(8,128)(2,1)S(1)}, bf16[256,1024]{1,0:T(8,128)(2,1)S(1)}, u32[]{:S(2)}, u32[]{:S(2)}) collective-permute-start(bf16[256,1024]{1,0:T(8,128)(2,1)S(1)} %slice.142), channel_id=1, source_target_pairs={{0,8},{4,12},{8,16},{12,20},{16,24},{20,28},{24,0},{28,4},{1,9},{5... | collective-permute-start | bytes 1572872 | tf_op jit(solution)/shard_map/ppermute | solution.py:58
  176.9 34.5 %collective-permute-start.41 = (bf16[256,1024]{1,0:T(8,128)(2,1)S(1)}, bf16[256,1024]{1,0:T(8,128)(2,1)S(1)}, u32[]{:S(2)}, u32[]{:S(2)}) collective-permute-start(bf16[256,1024]{1,0:T(8,128)(2,1)S(1)} %slice.141), channel_id=1, source_target_pairs={{0,4},{4,0},{8,12},{12,8},{16,20},{20,16},{24,28},{28,24},{1,5},{5... | collective-permute-start | bytes 1572872 | tf_op jit(solution)/shard_map/ppermute | solution.py:58
  196.3 22.5 %collective-permute-start.27 = (bf16[256,1024]{1,0:T(8,128)(2,1)S(1)}, bf16[256,1024]{1,0:T(8,128)(2,1)S(1)}, u32[]{:S(2)}, u32[]{:S(2)}) collective-permute-start(bf16[256,1024]{1,0:T(8,128)(2,1)S(1)} %slice.140), channel_id=1, source_target_pairs={{0,8},{4,12},{8,16},{12,20},{16,24},{20,28},{24,0},{28,4},{1,9},{5... | collective-permute-start | bytes 1572872 | tf_op jit(solution)/shard_map/ppermute | solution.py:58
  199.4 20.3 %collective-permute-start.26 = (bf16[256,1024]{1,0:T(8,128)(2,1)S(1)}, bf16[256,1024]{1,0:T(8,128)(2,1)S(1)}, u32[]{:S(2)}, u32[]{:S(2)}) collective-permute-start(bf16[256,1024]{1,0:T(8,128)(2,1)S(1)} %slice.139), channel_id=1, source_target_pairs={{0,4},{4,0},{8,12},{12,8},{16,20},{20,16},{24,28},{28,24},{1,5},{5... | collective-permute-start | bytes 1572872 | tf_op jit(solution)/shard_map/ppermute | solution.py:58
  210.6 117.4 %collective-permute-start.35 = (bf16[256,2048]{1,0:T(8,128)(2,1)}, bf16[256,2048]{1,0:T(8,128)(2,1)S(1)}, u32[]{:S(2)}, u32[]{:S(2)}) collective-permute-start(bf16[256,2048]{1,0:T(8,128)(2,1)} %get-tuple-element.67.refs_4_), channel_id=1, source_target_pairs={{0,4},{4,0},{8,12},{12,8},{16,20},{20,16},{24,28},{28,24},{1,5},{5... | collective-permute-start | bytes 3145736 | tf_op jit(solution)/shard_map/ppermute | solution.py:58
  211.4 52.4 %collective-permute-start.20 = (bf16[256,2048]{1,0:T(8,128)(2,1)}, bf16[256,2048]{1,0:T(8,128)(2,1)}, u32[]{:S(2)}, u32[]{:S(2)}) collective-permute-start(bf16[256,2048]{1,0:T(8,128)(2,1)} %get-tuple-element.66.refs_4_), channel_id=1, source_target_pairs={{0,4},{4,0},{8,12},{12,8},{16,20},{20,16},{24,28},{28,24},{1,5},{5... | collective-permute-start | bytes 3145736 | tf_op jit(solution)/shard_map/ppermute | solution.py:58
  218.9 109.1 %collective-permute-start.37 = (bf16[256,2048]{1,0:T(8,128)(2,1)}, bf16[256,2048]{1,0:T(8,128)(2,1)}, u32[]{:S(2)}, u32[]{:S(2)}) collective-permute-start(bf16[256,2048]{1,0:T(8,128)(2,1)} %collective-permute-done.36.refs_6_), channel_id=1, source_target_pairs={{0,4},{4,0},{8,12},{12,8},{16,20},{20,16},{24,28},{28,24},{1,5},{5... | collective-permute-start | bytes 3145736 | tf_op jit(solution)/shard_map/ppermute | solution.py:58
  219.7 85.8 %collective-permute-start.22 = (bf16[256,2048]{1,0:T(8,128)(2,1)}, bf16[256,2048]{1,0:T(8,128)(2,1)S(1)}, u32[]{:S(2)}, u32[]{:S(2)}) collective-permute-start(bf16[256,2048]{1,0:T(8,128)(2,1)} %collective-permute-done.21.refs_6_), channel_id=1, source_target_pairs={{0,4},{4,0},{8,12},{12,8},{16,20},{20,16},{24,28},{28,24},{1,5},{5... | collective-permute-start | bytes 3145736 | tf_op jit(solution)/shard_map/ppermute | solution.py:58
  353.4 21.7 %collective-permute-start.43 = (f32[512,256]{1,0:T(8,128)S(1)}, f32[512,256]{1,0:T(8,128)S(1)}, u32[]{:S(2)}, u32[]{:S(2)}) collective-permute-start(f32[512,256]{1,0:T(8,128)S(1)} %get-tuple-element.62), channel_id=1, source_target_pairs={{0,4},{4,0},{8,12},{12,8},{16,20},{20,16},{24,28},{28,24},{1,5},{5... | collective-permute-start | bytes 1572872 | tf_op jit(solution)/shard_map/ppermute | solution.py:58
  356.8 17.0 %collective-permute-start.15 = (f32[128,512]{1,0:T(8,128)S(1)}, f32[128,512]{1,0:T(8,128)S(1)}, u32[]{:S(2)}, u32[]{:S(2)}) collective-permute-start(f32[128,512]{1,0:T(8,128)S(1)} %fusion.46), channel_id=1, source_target_pairs={{0,4},{4,0},{8,12},{12,8},{16,20},{20,16},{24,28},{28,24},{1,5},{5... | collective-permute-start | bytes 786440 | tf_op jit(solution)/shard_map/ppermute | solution.py:104
  359.0 28.1 %collective-permute-start.28 = (f32[512,256]{1,0:T(8,128)S(1)}, f32[512,256]{1,0:T(8,128)S(1)}, u32[]{:S(2)}, u32[]{:S(2)}) collective-permute-start(f32[512,256]{1,0:T(8,128)S(1)} %get-tuple-element.58), channel_id=1, source_target_pairs={{0,4},{4,0},{8,12},{12,8},{16,20},{20,16},{24,28},{28,24},{1,5},{5... | collective-permute-start | bytes 1572872 | tf_op jit(solution)/shard_map/ppermute | solution.py:58
  373.9 12.5 %collective-permute-start.16 = (f32[128,512]{1,0:T(8,128)S(1)}, f32[128,512]{1,0:T(8,128)S(1)}, u32[]{:S(2)}, u32[]{:S(2)}) collective-permute-start(f32[128,512]{1,0:T(8,128)S(1)} %add.197), channel_id=1, source_target_pairs={{0,8},{4,12},{8,0},{12,4},{16,24},{20,28},{24,16},{28,20},{1,9},{5... | collective-permute-start | bytes 786440 | tf_op jit(solution)/shard_map/ppermute | solution.py:104
  374.0 48.4 %collective-permute-start.45 = (f32[512,256]{1,0:T(8,128)}, f32[512,256]{1,0:T(8,128)}, u32[]{:S(2)}, u32[]{:S(2)}) collective-permute-start(f32[512,256]{1,0:T(8,128)} %get-tuple-element.61), channel_id=1, source_target_pairs={{0,4},{4,0},{8,12},{12,8},{16,20},{20,16},{24,28},{28,24},{1,5},{5... | collective-permute-start | bytes 1572872 | tf_op jit(solution)/shard_map/ppermute | solution.py:58
  377.1 46.4 %collective-permute-start.44 = (f32[512,256]{1,0:T(8,128)}, f32[512,256]{1,0:T(8,128)}, u32[]{:S(2)}, u32[]{:S(2)}) collective-permute-start(f32[512,256]{1,0:T(8,128)} %dynamic-slice_add_fusion), channel_id=1, source_target_pairs={{0,8},{4,12},{8,16},{12,20},{16,24},{20,28},{24,0},{28,4},{1,9},{5... | collective-permute-start | bytes 1572872 | tf_op jit(solution)/shard_map/ppermute | solution.py:58
  386.4 33.2 %collective-permute-start.17 = (f32[128,512]{1,0:T(8,128)S(1)}, f32[128,512]{1,0:T(8,128)}, u32[]{:S(2)}, u32[]{:S(2)}) collective-permute-start(f32[128,512]{1,0:T(8,128)S(1)} %add.198), channel_id=1, source_target_pairs={{0,16},{4,20},{8,24},{12,28},{16,0},{20,4},{24,8},{28,12},{1,17},{... | collective-permute-start | bytes 786440 | tf_op jit(solution)/shard_map/ppermute | solution.py:104
  386.5 40.4 %collective-permute-start.30 = (f32[512,256]{1,0:T(8,128)}, f32[512,256]{1,0:T(8,128)}, u32[]{:S(2)}, u32[]{:S(2)}) collective-permute-start(f32[512,256]{1,0:T(8,128)} %get-tuple-element.57), channel_id=1, source_target_pairs={{0,4},{4,0},{8,12},{12,8},{16,20},{20,16},{24,28},{28,24},{1,5},{5... | collective-permute-start | bytes 1572872 | tf_op jit(solution)/shard_map/ppermute | solution.py:58
  388.0 38.9 %collective-permute-start.29 = (f32[512,256]{1,0:T(8,128)}, f32[512,256]{1,0:T(8,128)}, u32[]{:S(2)}, u32[]{:S(2)}) collective-permute-start(f32[512,256]{1,0:T(8,128)} %dynamic-slice_add_fusion.1), channel_id=1, source_target_pairs={{0,8},{4,12},{8,16},{12,20},{16,24},{20,28},{24,0},{28,4},{1,9},{5... | collective-permute-start | bytes 1572872 | tf_op jit(solution)/shard_map/ppermute | solution.py:58
  419.7 12.3 %collective-permute-start.47 = (f32[512,256]{1,0:T(8,128)}, f32[512,256]{1,0:T(8,128)}, u32[]{:S(2)}, u32[]{:S(2)}) collective-permute-start(f32[512,256]{1,0:T(8,128)} %get-tuple-element.60), channel_id=1, source_target_pairs={{0,4},{4,0},{8,12},{12,8},{16,20},{20,16},{24,28},{28,24},{1,5},{5... | collective-permute-start | bytes 1572872 | tf_op jit(solution)/shard_map/ppermute | solution.py:58
  422.3 17.3 %collective-permute-start.32 = (f32[512,256]{1,0:T(8,128)}, f32[512,256]{1,0:T(8,128)}, u32[]{:S(2)}, u32[]{:S(2)}) collective-permute-start(f32[512,256]{1,0:T(8,128)} %get-tuple-element.56), channel_id=1, source_target_pairs={{0,4},{4,0},{8,12},{12,8},{16,20},{20,16},{24,28},{28,24},{1,5},{5... | collective-permute-start | bytes 1572872 | tf_op jit(solution)/shard_map/ppermute | solution.py:58
  426.9 11.3 %collective-permute-start.46 = (f32[512,256]{1,0:T(8,128)}, f32[512,256]{1,0:T(8,128)}, u32[]{:S(2)}, u32[]{:S(2)}) collective-permute-start(f32[512,256]{1,0:T(8,128)} %add_add_fusion.2), channel_id=1, source_target_pairs={{0,8},{4,12},{8,16},{12,20},{16,24},{20,28},{24,0},{28,4},{1,9},{5... | collective-permute-start | bytes 1572872 | tf_op jit(solution)/shard_map/ppermute | solution.py:58
  429.2 14.6 %collective-permute-start.31 = (f32[512,256]{1,0:T(8,128)}, f32[512,256]{1,0:T(8,128)}, u32[]{:S(2)}, u32[]{:S(2)}) collective-permute-start(f32[512,256]{1,0:T(8,128)} %add_add_fusion.5), channel_id=1, source_target_pairs={{0,8},{4,12},{8,16},{12,20},{16,24},{20,28},{24,0},{28,4},{1,9},{5... | collective-permute-start | bytes 1572872 | tf_op jit(solution)/shard_map/ppermute | solution.py:58
  430.1 58.8 %collective-permute-start.49 = (f32[512,256]{1,0:T(8,128)}, f32[512,256]{1,0:T(8,128)S(1)}, u32[]{:S(2)}, u32[]{:S(2)}) collective-permute-start(f32[512,256]{1,0:T(8,128)} %get-tuple-element.59), channel_id=1, source_target_pairs={{0,4},{4,0},{8,12},{12,8},{16,20},{20,16},{24,28},{28,24},{1,5},{5... | collective-permute-start | bytes 1572872 | tf_op jit(solution)/shard_map/ppermute | solution.py:58
  432.0 58.1 %collective-permute-start.34 = (f32[512,256]{1,0:T(8,128)}, f32[512,256]{1,0:T(8,128)S(1)}, u32[]{:S(2)}, u32[]{:S(2)}) collective-permute-start(f32[512,256]{1,0:T(8,128)} %get-tuple-element.55), channel_id=1, source_target_pairs={{0,4},{4,0},{8,12},{12,8},{16,20},{20,16},{24,28},{28,24},{1,5},{5... | collective-permute-start | bytes 1572872 | tf_op jit(solution)/shard_map/ppermute | solution.py:58
  439.7 49.3 %collective-permute-start.48 = (f32[512,256]{1,0:T(8,128)S(1)}, f32[512,256]{1,0:T(8,128)S(1)}, u32[]{:S(2)}, u32[]{:S(2)}) collective-permute-start(f32[512,256]{1,0:T(8,128)S(1)} %add_add_fusion.1), channel_id=1, source_target_pairs={{0,8},{4,12},{8,16},{12,20},{16,24},{20,28},{24,0},{28,4},{1,9},{5... | collective-permute-start | bytes 1572872 | tf_op jit(solution)/shard_map/ppermute | solution.py:58
  445.3 44.8 %collective-permute-start.33 = (f32[512,256]{1,0:T(8,128)S(1)}, f32[512,256]{1,0:T(8,128)S(1)}, u32[]{:S(2)}, u32[]{:S(2)}) collective-permute-start(f32[512,256]{1,0:T(8,128)S(1)} %add_add_fusion.4), channel_id=1, source_target_pairs={{0,8},{4,12},{8,16},{12,20},{16,24},{20,28},{24,0},{28,4},{1,9},{5... | collective-permute-start | bytes 1572872 | tf_op jit(solution)/shard_map/ppermute | solution.py:58
  510.1 11.5 %collective-permute-start.55 = (f16[528,512]{1,0:T(8,128)(2,1)S(1)}, f16[528,512]{1,0:T(8,128)(2,1)S(1)}, u32[]{:S(2)}, u32[]{:S(2)}) collective-permute-start(f16[528,512]{1,0:T(8,128)(2,1)S(1)} %pad_maximum_fusion.9), channel_id=1, source_target_pairs={{0,4},{4,0},{8,12},{12,8},{16,20},{20,16},{24,28},{28,24},{1,5},{5... | collective-permute-start | bytes 1622024 | tf_op jit(solution)/shard_map/ppermute | solution.py:58
  511.0 13.2 %collective-permute-start.56 = (f16[528,512]{1,0:T(8,128)(2,1)S(1)}, f16[528,512]{1,0:T(8,128)(2,1)S(1)}, u32[]{:S(2)}, u32[]{:S(2)}) collective-permute-start(f16[528,512]{1,0:T(8,128)(2,1)S(1)} %pad_maximum_fusion.9), channel_id=1, source_target_pairs={{0,8},{4,12},{8,16},{12,20},{16,24},{20,28},{24,0},{28,4},{1,9},{5... | collective-permute-start | bytes 1622024 | tf_op jit(solution)/shard_map/ppermute | solution.py:58
  525.4 11.9 %collective-permute-start.58 = (f16[528,512]{1,0:T(8,128)(2,1)S(1)}, f16[528,512]{1,0:T(8,128)(2,1)S(1)}, u32[]{:S(2)}, u32[]{:S(2)}) collective-permute-start(f16[528,512]{1,0:T(8,128)(2,1)S(1)} %collective-permute-done.56), channel_id=1, source_target_pairs={{0,8},{4,12},{8,16},{12,20},{16,24},{20,28},{24,0},{28,4},{1,9},{5... | collective-permute-start | bytes 1622024 | tf_op jit(solution)/shard_map/ppermute | solution.py:58
  537.3 10.4 %collective-permute-start.59 = (f16[528,512]{1,0:T(8,128)(2,1)S(1)}, f16[528,512]{1,0:T(8,128)(2,1)S(1)}, u32[]{:S(2)}, u32[]{:S(2)}) collective-permute-start(f16[528,512]{1,0:T(8,128)(2,1)S(1)} %collective-permute-done.58), channel_id=1, source_target_pairs={{0,4},{4,0},{8,12},{12,8},{16,20},{20,16},{24,28},{28,24},{1,5},{5... | collective-permute-start | bytes 1622024 | tf_op jit(solution)/shard_map/ppermute | solution.py:58
  538.1 12.1 %collective-permute-start.60 = (f16[528,512]{1,0:T(8,128)(2,1)S(1)}, f16[528,512]{1,0:T(8,128)(2,1)S(1)}, u32[]{:S(2)}, u32[]{:S(2)}) collective-permute-start(f16[528,512]{1,0:T(8,128)(2,1)S(1)} %collective-permute-done.58), channel_id=1, source_target_pairs={{0,8},{4,12},{8,16},{12,20},{16,24},{20,28},{24,0},{28,4},{1,9},{5... | collective-permute-start | bytes 1622024 | tf_op jit(solution)/shard_map/ppermute | solution.py:58
  (30 other events, 365.3 us)
